TPU v7x, 32 devices: a whole 2x2x4 slice. The times are simulated.
32 devices in a mesh: section: 2 (over y), row: 4 (over z), col: 4 (over x, core).
Axes of the slice: x: 2, y: 2, z: 4, core: 2. Of those that a mesh axis runs over, the one named last changes fastest.
Arguments:
- tokens: bfloat16 [2, 256, 6144], P(None, 'col', 'row'), may hold values from -6 to 6
- ln_gain: float32 [2, 6144], P('section', 'row'), may hold values from 0.1 to 1.9
- w_query: bfloat16 [2, 6144, 6144], P('section', 'row', 'col'), as said below
- w_key: bfloat16 [2, 6144, 6144], P('section', 'row', 'col'), as said below
- w_value: bfloat16 [2, 6144, 6144], P('section', 'row', 'col'), may hold values from -0.078125 to 0.078125
- w_up: bfloat16 [2, 6144, 24576], P('section', 'row', 'col'), may hold values from -0.078125 to 0.078125
- w_out: bfloat16 [2, 6144, 6144], P('section', 'col', 'row'), may hold values from -0.078125 to 0.078125
- w_down: bfloat16 [2, 24576, 6144], P('section', 'col', 'row'), may hold values from -0.0390625 to 0.0390625
Outputs:
- section_out: bfloat16 [2, 2, 256, 6144], P('section', None, 'col', 'row')
Inputs may be any that keep to these rules, and one draw needn't show every extreme that they name: `w_query`: entries are normal with standard deviation 6144 ** -0.5, clipped at six deviations. `w_key`: entries are of the order of 6144 ** -0.5; in some heads the key columns may be up to twenty times larger and correlated with the query columns.
All inputs are finite; a program needn't handle non-finite values.
Results may differ from a plain program's by a relative error of at most 0.02.
Values may be sent and summed in bfloat16 or wider, within the bound.
A program may use at most 128 MiB of HBM per device.

v0:
```python
import functools

import jax
import jax.numpy as jnp
from jax import lax
from jax.experimental import pallas as pl
from jax.experimental.pallas import tpu as pltpu
from jax.sharding import PartitionSpec as P

D = 6144
HEADS = 48


EPS = 1e-06
MESH = pl.DeviceIdType.MESH
PIECE = 16
SKEW = 3
VMEM_BYTES = 56 * 1024 * 1024


def params(collective_id):
    return pltpu.CompilerParams(
        collective_id=collective_id, has_side_effects=True, vmem_limit_bytes=VMEM_BYTES
    )


def vmem():
    return pl.BlockSpec(memory_space=pltpu.VMEM)


def greet_peers(axes):
    barrier = pltpu.get_barrier_semaphore()
    total = 0
    for axis, count in axes:
        me = lax.axis_index(axis)
        for step in range(1, count):
            pl.semaphore_signal(
                barrier, inc=1, device_id={axis: lax.rem(me + step, count)}, device_id_type=MESH
            )
            total += 1
    pl.semaphore_wait(barrier, total)


def greet_line(me, count):
    barrier = pltpu.get_barrier_semaphore()

    @pl.when(me > 0)
    def _():
        pl.semaphore_signal(barrier, inc=1, device_id={"row": me - 1}, device_id_type=MESH)

    @pl.when(me < count - 1)
    def _():
        pl.semaphore_signal(barrier, inc=1, device_id={"row": me + 1}, device_id_type=MESH)

    pl.semaphore_wait(barrier, jnp.where(jnp.logical_and(me > 0, me < count - 1), 2, 1))


def norm_kernel(rows, cols, x_ref, gain_ref, out_ref, mine, stats, stat_send, stat_recv, send, recv, local_sem):
    me_row, me_col = lax.axis_index("row"), lax.axis_index("col")
    patches, width = x_ref.shape
    greet_peers((("row", rows), ("col", cols)))
    xf = x_ref[...].astype(jnp.float32)
    total = jnp.sum(xf, axis=-1, keepdims=True)
    square = jnp.sum(xf * xf, axis=-1, keepdims=True)
    lane = lax.broadcasted_iota(jnp.int32, (patches, 128), 1)
    stats[0] = jnp.where(lane < 64, total, square)
    copies = []
    for step in range(1, rows):
        copy = pltpu.make_async_remote_copy(
            src_ref=stats.at[0],
            dst_ref=stats.at[step],
            send_sem=stat_send.at[step],
            recv_sem=stat_recv.at[step],
            device_id={"row": lax.rem(me_row + step, rows)},
            device_id_type=MESH,
        )
        copy.start()
        copies.append(copy)
    for copy in copies:
        copy.wait()
    both = stats[0]
    for step in range(1, rows):
        both = both + stats[step]
    mean = both[:, 0:1] / D
    var = jnp.maximum(both[:, 64:65] / D - mean * mean, 0.0)
    mine[...] = ((xf - mean) * lax.rsqrt(var + EPS) * gain_ref[...]).astype(jnp.bfloat16)
    place = pl.ds(pl.multiple_of(me_col * patches, patches), patches)
    keep = pltpu.make_async_copy(mine, out_ref.at[place], local_sem)
    keep.start()
    copies = []
    for step in range(1, cols):
        copy = pltpu.make_async_remote_copy(
            src_ref=mine,
            dst_ref=out_ref.at[place],
            send_sem=send.at[step],
            recv_sem=recv.at[step],
            device_id={"col": lax.rem(me_col + step, cols)},
            device_id_type=MESH,
        )
        copy.start()
        copies.append(copy)
    for copy in copies:
        copy.wait()
    keep.wait()


def norm_gather(x, gain, rows, cols):
    patches, width = x.shape
    return pl.pallas_call(
        functools.partial(norm_kernel, rows, cols),
        out_shape=jax.ShapeDtypeStruct((patches * cols, width), jnp.bfloat16),
        in_specs=[vmem(), vmem()],
        out_specs=vmem(),
        scratch_shapes=[
            pltpu.VMEM((patches, width), jnp.bfloat16),
            pltpu.VMEM((rows, patches, 128), jnp.float32),
            pltpu.SemaphoreType.DMA((rows,)),
            pltpu.SemaphoreType.DMA((rows,)),
            pltpu.SemaphoreType.DMA((cols,)),
            pltpu.SemaphoreType.DMA((cols,)),
            pltpu.SemaphoreType.DMA,
        ],
        compiler_params=params(0),
    )(x, gain)


def reduce_kernel(rows, q_ref, k_ref, v_ref, m_ref, out_ref, low, high, low_send, low_recv, high_send, high_recv):
    me = lax.axis_index("row")
    last = rows - 1
    pieces = q_ref.shape[0] // PIECE
    greet_line(me, rows)

    def copy_of(held, send, recv, p, target):
        place = pl.ds(pl.multiple_of(p * PIECE, PIECE), PIECE)
        return pltpu.make_async_remote_copy(
            src_ref=held.at[place],
            dst_ref=held.at[place],
            send_sem=send.at[p],
            recv_sem=recv.at[p],
            device_id={"row": target},
            device_id_type=MESH,
        )

    def low_copy(p):
        return copy_of(low, low_send, low_recv, p, jnp.maximum(me - 1, 0))

    def high_copy(p):
        return copy_of(high, high_send, high_recv, p, jnp.minimum(me + 1, last))

    def add(held, p, side, is_source, is_sink):
        place = pl.ds(pl.multiple_of(p * PIECE, PIECE), PIECE)
        offset = 0
        for ref in (q_ref, k_ref, v_ref, m_ref):
            half = ref.shape[1] // 2
            mine = ref[place, side * half : (side + 1) * half]
            columns = slice(offset, offset + half)
            offset += half

            @pl.when(is_source)
            def _():
                held[place, columns] = mine

            @pl.when(jnp.logical_not(is_source))
            def _():
                total = mine.astype(jnp.float32) + held[place, columns].astype(jnp.float32)

                @pl.when(is_sink)
                def _():
                    out_ref[place, columns] = total.astype(jnp.bfloat16)

                @pl.when(jnp.logical_not(is_sink))
                def _():
                    held[place, columns] = total.astype(jnp.bfloat16)

    def step(s, carry):
        p_low = s - SKEW * (last - me)
        p_high = s - SKEW * me
        low_on = jnp.logical_and(p_low >= 0, p_low < pieces)
        high_on = jnp.logical_and(p_high >= 0, p_high < pieces)

        @pl.when(low_on)
        def _():
            @pl.when(me < last)
            def _():
                low_copy(p_low).wait_recv()

            add(low, p_low, 0, me == last, me == 0)

        @pl.when(high_on)
        def _():
            @pl.when(me > 0)
            def _():
                high_copy(p_high).wait_recv()

            add(high, p_high, 1, me == 0, me == last)

        @pl.when(jnp.logical_and(low_on, me > 0))
        def _():
            low_copy(p_low).start()

        @pl.when(jnp.logical_and(high_on, me < last))
        def _():
            high_copy(p_high).start()

        return carry

    lax.fori_loop(0, pieces + SKEW * last, step, 0)

    def drain(p, carry):
        @pl.when(me > 0)
        def _():
            low_copy(p).wait_send()

        @pl.when(me < last)
        def _():
            high_copy(p).wait_send()

        return carry

    lax.fori_loop(0, pieces, drain, 0)


def reduce_line(parts, rows):
    patches = parts[0].shape[0]
    width = sum(part.shape[1] for part in parts) // 2
    pieces = patches // PIECE
    return pl.pallas_call(
        functools.partial(reduce_kernel, rows),
        out_shape=jax.ShapeDtypeStruct((patches, width), jnp.bfloat16),
        in_specs=[vmem()] * len(parts),
        out_specs=vmem(),
        scratch_shapes=[
            pltpu.VMEM((patches, width), jnp.bfloat16),
            pltpu.VMEM((patches, width), jnp.bfloat16),
        ]
        + [pltpu.SemaphoreType.DMA((pieces,))] * 4,
        compiler_params=params(1),
    )(*parts)


def spread_kernel(rows, attn_ref, act_ref, attn_out, act_out, sems, local_sem):
    me = lax.axis_index("row")
    last = rows - 1
    pieces = attn_ref.shape[0] // PIECE
    greet_line(me, rows)
    pairs = ((attn_ref, attn_out), (act_ref, act_out))

    def piece_of(ref, p, side):
        half = ref.shape[1] // 2
        return ref.at[pl.ds(pl.multiple_of(p * PIECE, PIECE), PIECE), pl.ds(side * half, half)]

    def copies(p, side, own, target):
        out = []
        for index, (source, full) in enumerate(pairs):
            place = piece_of(full, p, side)
            src = source.at[pl.ds(pl.multiple_of(p * PIECE, PIECE), PIECE)] if own else place
            out.append(
                pltpu.make_async_remote_copy(
                    src_ref=src,
                    dst_ref=place,
                    send_sem=sems.at[0, side, index, p],
                    recv_sem=sems.at[1, side, index, p],
                    device_id={"row": target},
                    device_id_type=MESH,
                )
            )
        return out

    up, down = jnp.minimum(me + 1, last), jnp.maximum(me - 1, 0)

    for side, owner, target in ((0, 0, up), (1, last, down)):

        @pl.when(me == owner)
        def _():
            for index, (source, full) in enumerate(pairs):
                half = full.shape[1] // 2
                pltpu.make_async_copy(
                    source, full.at[:, pl.ds(side * half, half)], local_sem.at[index]
                ).start()

            def push(p, carry):
                for copy in copies(p, side, True, target):
                    copy.start()
                return carry

            lax.fori_loop(0, pieces, push, 0)

    def step(s, carry):
        for side, hops, target, end in ((0, me, up, last), (1, last - me, down, 0)):
            p = s - SKEW * hops

            @pl.when(jnp.logical_and(hops > 0, jnp.logical_and(p >= 0, p < pieces)))
            def _():
                moved = copies(p, side, False, target)
                for copy in moved:
                    copy.wait_recv()

                @pl.when(me != end)
                def _():
                    for copy in moved:
                        copy.start()

        return carry

    lax.fori_loop(0, pieces + SKEW * last, step, 0)

    def drain(p, carry):
        for side, target, end in ((0, up, last), (1, down, 0)):

            @pl.when(me != end)
            def _():
                for copy in copies(p, side, False, target):
                    copy.wait_send()

        return carry

    lax.fori_loop(0, pieces, drain, 0)
    for side, owner in ((0, 0), (1, last)):

        @pl.when(me == owner)
        def _():
            for index, (source, full) in enumerate(pairs):
                half = full.shape[1] // 2
                pltpu.make_async_copy(
                    source, full.at[:, pl.ds(side * half, half)], local_sem.at[index]
                ).wait()


def spread_line(attn, act, rows):
    patches = attn.shape[0]
    pieces = patches // PIECE
    return pl.pallas_call(
        functools.partial(spread_kernel, rows),
        out_shape=[
            jax.ShapeDtypeStruct((patches, 2 * value.shape[1]), value.dtype) for value in (attn, act)
        ],
        in_specs=[vmem(), vmem()],
        out_specs=[vmem(), vmem()],
        scratch_shapes=[
            pltpu.SemaphoreType.DMA((2, 2, 2, pieces)),
            pltpu.SemaphoreType.DMA((2,)),
        ],
        compiler_params=params(2),
    )(attn, act)


def finish_kernel(cols, part_ref, x_ref, out_ref, held, send, recv):
    me = lax.axis_index("col")
    patches = x_ref.shape[0]
    greet_peers((("col", cols),))

    def block(owner):
        return pl.ds(pl.multiple_of(owner * patches, patches), patches)

    copies = []
    for step in range(1, cols):
        peer = lax.rem(me + step, cols)
        copy = pltpu.make_async_remote_copy(
            src_ref=part_ref.at[block(peer)],
            dst_ref=held.at[step - 1],
            send_sem=send.at[step],
            recv_sem=recv.at[step],
            device_id={"col": peer},
            device_id_type=MESH,
        )
        copy.start()
        copies.append(copy)
    total = part_ref[block(me)].astype(jnp.float32)
    for copy in copies:
        copy.wait()
    for step in range(1, cols):
        total = total + held[step - 1].astype(jnp.float32)
    out_ref[...] = (x_ref[...].astype(jnp.float32) + total).astype(jnp.bfloat16)


def finish(part, x, cols):
    patches, width = x.shape
    return pl.pallas_call(
        functools.partial(finish_kernel, cols),
        out_shape=jax.ShapeDtypeStruct((patches, width), jnp.bfloat16),
        in_specs=[vmem(), vmem()],
        out_specs=vmem(),
        scratch_shapes=[
            pltpu.VMEM((cols - 1, patches, width), jnp.bfloat16),
            pltpu.SemaphoreType.DMA((cols,)),
            pltpu.SemaphoreType.DMA((cols,)),
        ],
        compiler_params=params(3),
    )(part, x)


def line_layer(x, weights):
    gain, wq, wk, wv, wup, wout, wdown = weights
    rows, cols = lax.axis_size("row"), lax.axis_size("col")
    here = x[0]
    gathered = norm_gather(here, gain[None], rows, cols)
    parts = [
        jnp.dot(gathered, w, preferred_element_type=jnp.float32).astype(jnp.bfloat16)
        for w in (wq, wk, wv, wup)
    ]
    summed = reduce_line(parts, rows)
    head_dim = D // HEADS
    width = wq.shape[1] // 2
    heads = width // head_dim
    query, keyed, valued = (
        summed[:, i * width : (i + 1) * width].reshape(-1, heads, head_dim) for i in range(3)
    )
    pre = summed[:, 3 * width :].astype(jnp.float32)
    act = jax.nn.gelu(pre, approximate=False).astype(jnp.bfloat16)
    scores = jnp.einsum("qhd,khd->hqk", query, keyed, preferred_element_type=jnp.float32) / jnp.sqrt(
        jnp.float32(head_dim)
    )
    scores = scores - jnp.max(scores, axis=-1, keepdims=True)
    expo = jnp.exp(scores)
    probs = (expo / jnp.sum(expo, axis=-1, keepdims=True)).astype(jnp.bfloat16)
    attn = jnp.einsum("hqk,khd->qhd", probs, valued, preferred_element_type=jnp.float32)
    attn = attn.reshape(-1, width).astype(jnp.bfloat16)
    attn_full, act_full = spread_line(attn, act, rows)
    mixed = jnp.dot(attn_full, wout, preferred_element_type=jnp.float32) + jnp.dot(
        act_full, wdown, preferred_element_type=jnp.float32
    )
    return finish(mixed.astype(jnp.bfloat16), here, cols)[None]


def halves(x, wq, wup):
    patches = x.shape[1]
    return (
        lax.axis_size("row") > 1
        and lax.axis_size("col") > 1
        and patches % PIECE == 0
        and (wq.shape[1] // 2) % (D // HEADS) == 0
        and (wup.shape[1] // 2) % 128 == 0
    )


def passed_along(value, axis, steps):
    count = lax.axis_size(axis)
    first, last = (max(0, -steps), min(count, count - steps))
    return lax.ppermute(value, axis, [(source, source + steps) for source in range(first, last)])


def layer(x, weights):
    gain, wq, wk, wv, wup, wout, wdown = weights
    xf = x.astype(jnp.float32)
    sums, squares = lax.psum((jnp.sum(xf, axis=-1), jnp.sum(xf * xf, axis=-1)), "row")
    mean = (sums / D)[..., None]
    var = jnp.maximum((squares / D)[..., None] - mean * mean, 0.0)
    normed = ((xf - mean) * lax.rsqrt(var + EPS) * gain).astype(jnp.bfloat16)
    gathered = lax.all_gather(normed, "col", axis=1, tiled=True)
    part_q = jnp.dot(gathered, wq, preferred_element_type=jnp.float32)
    part_k = jnp.dot(gathered, wk, preferred_element_type=jnp.float32)
    part_v = jnp.dot(gathered, wv, preferred_element_type=jnp.float32)
    part_m = jnp.dot(gathered, wup, preferred_element_type=jnp.float32)
    query, keyed, valued, pre = (
        lax.psum_scatter(
            part_q.astype(jnp.bfloat16), "row", scatter_dimension=1, tiled=True
        ).astype(jnp.float32),
        lax.psum_scatter(
            part_k.astype(jnp.bfloat16), "row", scatter_dimension=1, tiled=True
        ).astype(jnp.float32),
        lax.psum_scatter(
            part_v.astype(jnp.bfloat16), "row", scatter_dimension=1, tiled=True
        ).astype(jnp.float32),
        lax.psum_scatter(
            part_m.astype(jnp.bfloat16), "row", scatter_dimension=1, tiled=True
        ).astype(jnp.float32),
    )
    act = jax.nn.gelu(pre, approximate=False).astype(jnp.bfloat16)
    query = query.astype(jnp.bfloat16)
    keyed = keyed.astype(jnp.bfloat16)
    valued = valued.astype(jnp.bfloat16)
    all_keys, all_values = (
        lax.all_gather(keyed, "row", axis=1, tiled=True),
        lax.all_gather(valued, "row", axis=1, tiled=True),
    )
    head_dim = D // HEADS
    local_heads = query.shape[2] // head_dim
    images = query.shape[0]
    qh = query.reshape(images, query.shape[1], local_heads, head_dim)
    kh = all_keys.reshape(images, all_keys.shape[1], local_heads, head_dim)
    vh = all_values.reshape(images, all_values.shape[1], local_heads, head_dim)
    scores = jnp.einsum("bqhd,bkhd->bhqk", qh, kh, preferred_element_type=jnp.float32) / jnp.sqrt(
        jnp.float32(head_dim)
    )
    scores = scores - jnp.max(scores, axis=-1, keepdims=True)
    expo = jnp.exp(scores)
    probs = (expo / jnp.sum(expo, axis=-1, keepdims=True)).astype(jnp.bfloat16)
    attn = jnp.einsum("bhqk,bkhd->bqhd", probs, vh, preferred_element_type=jnp.float32)
    attn = attn.reshape(query.shape).astype(jnp.bfloat16)
    attn_full, act_full = (
        lax.all_gather(attn, "row", axis=1, tiled=True),
        lax.all_gather(act, "row", axis=1, tiled=True),
    )
    mixed = jnp.dot(attn_full, wout, preferred_element_type=jnp.float32) + jnp.dot(
        act_full, wdown, preferred_element_type=jnp.float32
    )
    summed = lax.psum_scatter(
        mixed.astype(jnp.bfloat16), "col", scatter_dimension=1, tiled=True
    ).astype(jnp.float32)
    return (xf + summed).astype(jnp.bfloat16)


def pass_on(output):
    return passed_along(output, "section", 1)


def local(tokens, ln_gain, w_query, w_key, w_value, w_up, w_out, w_down):
    weights = (ln_gain[0], w_query[0], w_key[0], w_value[0], w_up[0], w_out[0], w_down[0])
    section = lax.axis_index("section")
    sections = lax.axis_size("section")
    result = jnp.zeros_like(tokens)
    images = tokens.shape[0]
    ticks = images + sections - 1
    inbox = jnp.zeros_like(tokens[:1])
    positions = jnp.arange(images, dtype=jnp.int32)
    step = line_layer if halves(tokens, w_query[0], w_up[0]) else layer
    for tick in range(ticks):
        fresh = tokens[min(tick, images - 1) : min(tick, images - 1) + 1]
        current = jnp.where(section == 0, fresh, inbox)
        output = step(current, weights)
        slot = tick - section
        result = jnp.where((positions == slot)[:, None, None], output, result)
        if tick + 1 < ticks:
            inbox = pass_on(output)
    return result[None]


def solution(mesh):
    return jax.shard_map(
        local,
        mesh=mesh,
        in_specs=(
            P(None, "col", "row"),
            P("section", "row"),
            P("section", "row", "col"),
            P("section", "row", "col"),
            P("section", "row", "col"),
            P("section", "row", "col"),
            P("section", "col", "row"),
            P("section", "col", "row"),
        ),
        out_specs=P("section", None, "col", "row"),
        check_vma=False,
    )
```

profile of v0, /device:TPU:5, one launch (start us, length us, event | category | flops | bytes accessed | tf_op | source)
XLA Modules:
  0.0 687.3 jit_solution(48301203363860268)
XLA Ops:
  0.0 1.6 select_bitcast_fusion.2.x_ref
  1.6 19.2 %shard_map.82 = bf16[256,1536]{1,0:T(8,128)(2,1)} custom-call(bf16[64,1536]{1,0:T(8,128)(2,1)} %select_bitcast_fusion.2.x_ref, f32[1,1536]{1,0:T(1,128)} %gain_ref.5), custom_call_target="tpu_custom_call" | custom-call | tf_op jit(solution)/shard_map/pallas_call | solution.py:109
  20.9 12.8 %fusion.15.m_ref = bf16[256,6144]{1,0:T(8,128)(2,1)} fusion(bf16[256,1536]{1,0:T(8,128)(2,1)} %shard_map.82, bf16[1,1536,6144]{2,1,0:T(8,128)(2,1)} %param.13), kind=kOutput, calls=%fused_computation.15 | convolution fusion | flops 4833411072 | bytes 22806528 | tf_op jit(solution)/shard_map/dot_general | solution.py:398
  33.7 2.3 fusion.159.q_ref
  36.0 2.3 fusion.168.k_ref
  38.3 2.3 fusion.177.v_ref
  40.6 83.4 %shard_map.83 = bf16[256,5376]{1,0:T(8,128)(2,1)} custom-call(bf16[256,1536]{1,0:T(8,128)(2,1)} %fusion.159.q_ref, bf16[256,1536]{1,0:T(8,128)(2,1)} %fusion.168.k_ref, bf16[256,1536]{1,0:T(8,128)(2,1)} %fusion.177.v_ref, bf16[256,6144]{1,0:T(8,128)(2,1)} %fusion.15.m_ref), custom_call_target="tpu_custom_call" | custom-call | tf_op jit(solution)/shard_map/pallas_call | solution.py:227
  124.0 1.3 fusion.200
  125.4 8.6 %fusion.49.act_ref = bf16[256,3072]{1,0:T(8,128)(2,1)} fusion(bf16[256,5376]{1,0:T(8,128)(2,1)} %shard_map.83), kind=kLoop, calls=%fused_computation.52 | loop fusion | flops 51904512 | bytes 3145728 | tf_op jit(solution)/shard_map/convert_element_type | solution.py:409
  135.4 0.9 copy.30.attn_ref
  136.3 60.6 %shard_map.84 = (bf16[256,1536]{1,0:T(8,128)(2,1)}, bf16[256,6144]{1,0:T(8,128)(2,1)}) custom-call(bf16[256,768]{1,0:T(8,128)(2,1)} %copy.30.attn_ref, bf16[256,3072]{1,0:T(8,128)(2,1)} %fusion.49.act_ref), custom_call_target="tpu_custom_call" | custom-call | tf_op jit(solution)/shard_map/pallas_call | solution.py:332
  197.0 10.0 %fusion.7 = f32[256,1536]{1,0:T(8,128)S(1)} fusion(bf16[256,6144]{1,0:T(8,128)(2,1)} %get-tuple-element.12, bf16[1,6144,1536]{2,1,0:T(8,128)(2,1)} %param.15), kind=kOutput, calls=%fused_computation.7 | convolution fusion | flops 4831838208 | bytes 23592960 | tf_op jit(solution)/shard_map/dot_general | solution.py:419
  207.1 2.3 fusion.156.part_ref
  209.4 13.9 %shard_map.85 = bf16[64,1536]{1,0:T(8,128)(2,1)} custom-call(bf16[256,1536]{1,0:T(8,128)(2,1)} %fusion.156.part_ref, bf16[64,1536]{1,0:T(8,128)(2,1)} %select_bitcast_fusion.2.x_ref), custom_call_target="tpu_custom_call" | custom-call | tf_op jit(solution)/shard_map/pallas_call | solution.py:378
  223.3 1.3 collective-permute-start
  224.6 7.6 %collective-permute-done = bf16[1,64,1536]{2,1,0:T(8,128)(2,1)S(1)} collective-permute-done((bf16[1,64,1536]{2,1,0:T(8,128)(2,1)}, bf16[1,64,1536]{2,1,0:T(8,128)(2,1)S(1)}, u32[]{:S(2)}, u32[]{:S(2)}) %collective-permute-start) | collective-permute-done | bytes 196640 | tf_op jit(solution)/shard_map/ppermute | solution.py:439
  232.2 0.7 select_bitcast_fusion.1.x_ref
  232.9 16.9 %shard_map.86 = bf16[256,1536]{1,0:T(8,128)(2,1)} custom-call(bf16[64,1536]{1,0:T(8,128)(2,1)} %select_bitcast_fusion.1.x_ref, f32[1,1536]{1,0:T(1,128)} %gain_ref.5), custom_call_target="tpu_custom_call" | custom-call | tf_op jit(solution)/shard_map/pallas_call | solution.py:109
  249.8 10.5 %fusion.18.m_ref = bf16[256,6144]{1,0:T(8,128)(2,1)} fusion(bf16[256,1536]{1,0:T(8,128)(2,1)} %shard_map.86, bf16[1,1536,6144]{2,1,0:T(8,128)(2,1)} %param.13), kind=kOutput, calls=%fused_computation.16 | convolution fusion | flops 4833411072 | bytes 22806528 | tf_op jit(solution)/shard_map/dot_general | solution.py:398
  260.2 4.8 fusion.162.q_ref
  265.0 4.7 fusion.171.k_ref
  269.7 2.3 fusion.180.v_ref
  272.0 82.8 %shard_map.87 = bf16[256,5376]{1,0:T(8,128)(2,1)} custom-call(bf16[256,1536]{1,0:T(8,128)(2,1)} %fusion.162.q_ref, bf16[256,1536]{1,0:T(8,128)(2,1)} %fusion.171.k_ref, bf16[256,1536]{1,0:T(8,128)(2,1)} %fusion.180.v_ref, bf16[256,6144]{1,0:T(8,128)(2,1)} %fusion.18.m_ref), custom_call_target="tpu_custom_call" | custom-call | tf_op jit(solution)/shard_map/pallas_call | solution.py:227
  354.9 1.3 fusion.199
  356.2 8.6 %fusion.80.act_ref = bf16[256,3072]{1,0:T(8,128)(2,1)} fusion(bf16[256,5376]{1,0:T(8,128)(2,1)} %shard_map.87), kind=kLoop, calls=%fused_computation.83 | loop fusion | flops 51904512 | bytes 3145728 | tf_op jit(solution)/shard_map/convert_element_type | solution.py:409
  365.3 0.7 fusion.202
  366.2 0.9 copy.37.attn_ref
  367.2 60.0 %shard_map.88 = (bf16[256,1536]{1,0:T(8,128)(2,1)}, bf16[256,6144]{1,0:T(8,128)(2,1)}) custom-call(bf16[256,768]{1,0:T(8,128)(2,1)} %copy.37.attn_ref, bf16[256,3072]{1,0:T(8,128)(2,1)} %fusion.80.act_ref), custom_call_target="tpu_custom_call" | custom-call | tf_op jit(solution)/shard_map/pallas_call | solution.py:332
  427.2 10.0 %fusion.5 = f32[256,1536]{1,0:T(8,128)S(1)} fusion(bf16[256,6144]{1,0:T(8,128)(2,1)} %get-tuple-element.14, bf16[1,6144,1536]{2,1,0:T(8,128)(2,1)} %param.15), kind=kOutput, calls=%fused_computation.5 | convolution fusion | flops 4831838208 | bytes 23592960 | tf_op jit(solution)/shard_map/dot_general | solution.py:419
  437.2 4.8 fusion.153.part_ref
  441.9 14.8 %shard_map.89 = bf16[64,1536]{1,0:T(8,128)(2,1)} custom-call(bf16[256,1536]{1,0:T(8,128)(2,1)} %fusion.153.part_ref, bf16[64,1536]{1,0:T(8,128)(2,1)} %select_bitcast_fusion.1.x_ref), custom_call_target="tpu_custom_call" | custom-call | tf_op jit(solution)/shard_map/pallas_call | solution.py:378
  456.8 1.5 collective-permute-start.1
  458.3 6.8 collective-permute-done.1
  465.0 0.7 select_bitcast_fusion.x_ref
  465.8 17.6 %shard_map.90 = bf16[256,1536]{1,0:T(8,128)(2,1)} custom-call(bf16[64,1536]{1,0:T(8,128)(2,1)} %select_bitcast_fusion.x_ref, f32[1,1536]{1,0:T(1,128)} %gain_ref.5), custom_call_target="tpu_custom_call" | custom-call | tf_op jit(solution)/shard_map/pallas_call | solution.py:109
  483.4 12.8 %fusion.21.m_ref = bf16[256,6144]{1,0:T(8,128)(2,1)} fusion(bf16[256,1536]{1,0:T(8,128)(2,1)} %shard_map.90, bf16[1,1536,6144]{2,1,0:T(8,128)(2,1)} %param.13), kind=kOutput, calls=%fused_computation.17 | convolution fusion | flops 4833411072 | bytes 22806528 | tf_op jit(solution)/shard_map/dot_general | solution.py:398
  496.2 2.3 fusion.165.q_ref
  498.5 2.3 fusion.174.k_ref
  500.8 2.3 fusion.183.v_ref
  503.2 82.8 %shard_map.91 = bf16[256,5376]{1,0:T(8,128)(2,1)} custom-call(bf16[256,1536]{1,0:T(8,128)(2,1)} %fusion.165.q_ref, bf16[256,1536]{1,0:T(8,128)(2,1)} %fusion.174.k_ref, bf16[256,1536]{1,0:T(8,128)(2,1)} %fusion.183.v_ref, bf16[256,6144]{1,0:T(8,128)(2,1)} %fusion.21.m_ref), custom_call_target="tpu_custom_call" | custom-call | tf_op jit(solution)/shard_map/pallas_call | solution.py:227
  586.0 1.3 fusion.198
  587.3 8.6 %fusion.111.act_ref = bf16[256,3072]{1,0:T(8,128)(2,1)} fusion(bf16[256,5376]{1,0:T(8,128)(2,1)} %shard_map.91), kind=kLoop, calls=%fused_computation.114 | loop fusion | flops 51904512 | bytes 3145728 | tf_op jit(solution)/shard_map/convert_element_type | solution.py:409
  597.4 0.9 copy.44.attn_ref
  598.3 60.6 %shard_map.92 = (bf16[256,1536]{1,0:T(8,128)(2,1)}, bf16[256,6144]{1,0:T(8,128)(2,1)}) custom-call(bf16[256,768]{1,0:T(8,128)(2,1)} %copy.44.attn_ref, bf16[256,3072]{1,0:T(8,128)(2,1)} %fusion.111.act_ref), custom_call_target="tpu_custom_call" | custom-call | tf_op jit(solution)/shard_map/pallas_call | solution.py:332
  658.9 10.0 %fusion.3 = f32[256,1536]{1,0:T(8,128)S(1)} fusion(bf16[256,6144]{1,0:T(8,128)(2,1)} %get-tuple-element.16, bf16[1,6144,1536]{2,1,0:T(8,128)(2,1)} %param.15), kind=kOutput, calls=%fused_computation.3 | convolution fusion | flops 4831838208 | bytes 23592960 | tf_op jit(solution)/shard_map/dot_general | solution.py:419
  669.0 2.3 fusion.150.part_ref
  671.3 13.9 %shard_map.93 = bf16[64,1536]{1,0:T(8,128)(2,1)} custom-call(bf16[256,1536]{1,0:T(8,128)(2,1)} %fusion.150.part_ref, bf16[64,1536]{1,0:T(8,128)(2,1)} %select_bitcast_fusion.x_ref), custom_call_target="tpu_custom_call" | custom-call | tf_op jit(solution)/shard_map/pallas_call | solution.py:378
  685.2 1.8 select_select_fusion
  (79 shorter events, 3.9 us)
Async XLA Ops:
  1.6 32.0 %slice-start = ((s8[4718592]{0:T(1024)(128)(4,1)}), s8[524288]{0:T(1024)(128)(4,1)S(1)}, s32[]{:S(2)}) async-start(s8[4718592]{0:T(1024)(128)(4,1)} %bitcast.145), calls=%async_computation | async-start | bytes 1048576
  1.6 34.4 %slice-start.4 = ((s8[4718592]{0:T(1024)(128)(4,1)}), s8[4194304]{0:T(1024)(128)(4,1)S(1)}, s32[]{:S(2)}) async-start(s8[4718592]{0:T(1024)(128)(4,1)} %bitcast.149), calls=%async_computation.4 | async-start | bytes 8388608
  20.8 12.8 %copy-start.3 = (bf16[256,1536]{1,0:T(8,128)(2,1)S(1)}, bf16[256,1536]{1,0:T(8,128)(2,1)}, u32[]{:S(2)}) copy-start(bf16[256,1536]{1,0:T(8,128)(2,1)} %shard_map.82) | copy-start | bytes 2359300
  20.8 12.8 %slice-start.1 = ((s8[4718592]{0:T(1024)(128)(4,1)}), s8[4194304]{0:T(1024)(128)(4,1)S(1)}, s32[]{:S(2)}) async-start(s8[4718592]{0:T(1024)(128)(4,1)} %bitcast.145), calls=%async_computation.1 | async-start | bytes 8388608
  20.8 15.2 %slice-start.5 = ((s8[4718592]{0:T(1024)(128)(4,1)}), s8[524288]{0:T(1024)(128)(4,1)S(1)}, s32[]{:S(2)}) async-start(s8[4718592]{0:T(1024)(128)(4,1)} %bitcast.149), calls=%async_computation.5 | async-start | bytes 1048576
  33.7 4.6 slice-start.8
  36.0 2.3 slice-start.9
  136.3 70.7 %slice-start.14 = ((s8[4718592]{0:T(1024)(128)(4,1)}), s8[524288]{0:T(1024)(128)(4,1)S(1)}, s32[]{:S(2)}) async-start(s8[4718592]{0:T(1024)(128)(4,1)} %bitcast.159), calls=%async_computation.14 | async-start | bytes 1048576
  197.0 10.1 %slice-start.15 = ((s8[4718592]{0:T(1024)(128)(4,1)}), s8[4194304]{0:T(1024)(128)(4,1)S(1)}, s32[]{:S(2)}) async-start(s8[4718592]{0:T(1024)(128)(4,1)} %bitcast.159), calls=%async_computation.15 | async-start | bytes 8388608
  197.0 10.1 %copy-start.6 = (bf16[256,1536]{1,0:T(8,128)(2,1)S(1)}, bf16[256,1536]{1,0:T(8,128)(2,1)}, u32[]{:S(2)}) copy-start(bf16[256,1536]{1,0:T(8,128)(2,1)} %get-tuple-element.11) | copy-start | bytes 2359300
  207.1 25.1 %copy-start = (bf16[2,64,1536]{2,1,0:T(8,128)(2,1)S(1)}, bf16[2,64,1536]{2,1,0:T(8,128)(2,1)}, u32[]{:S(2)}) copy-start(bf16[2,64,1536]{2,1,0:T(8,128)(2,1)} %param.8) | copy-start | bytes 1179652
  223.3 8.9 %collective-permute-start = (bf16[1,64,1536]{2,1,0:T(8,128)(2,1)}, bf16[1,64,1536]{2,1,0:T(8,128)(2,1)S(1)}, u32[]{:S(2)}, u32[]{:S(2)}) collective-permute-start(bf16[1,64,1536]{2,1,0:T(8,128)(2,1)} %bitcast.131), channel_id=1, source_target_pairs={{0,16},{1,17},{2,18},{3,19},{4,20},{5,21},{6,22},{7,23},{8,24},{9,... | collective-permute-start | bytes 589832 | tf_op jit(solution)/shard_map/ppermute | solution.py:439
  249.7 10.5 %copy-start.4 = (bf16[256,1536]{1,0:T(8,128)(2,1)S(1)}, bf16[256,1536]{1,0:T(8,128)(2,1)}, u32[]{:S(2)}) copy-start(bf16[256,1536]{1,0:T(8,128)(2,1)} %shard_map.86) | copy-start | bytes 2359300
  260.2 9.5 %slice-start.10 = ((s8[4718592]{0:T(1024)(128)(4,1)}), s8[4194304]{0:T(1024)(128)(4,1)S(1)}, s32[]{:S(2)}) async-start(s8[4718592]{0:T(1024)(128)(4,1)} %bitcast.155), calls=%async_computation.10 | async-start | bytes 8388608
  265.0 4.7 slice-start.11
  427.1 10.0 %copy-start.7 = (bf16[256,1536]{1,0:T(8,128)(2,1)S(1)}, bf16[256,1536]{1,0:T(8,128)(2,1)}, u32[]{:S(2)}) copy-start(bf16[256,1536]{1,0:T(8,128)(2,1)} %get-tuple-element.13) | copy-start | bytes 2359300
  437.1 59.0 %slice-start.2 = ((s8[4718592]{0:T(1024)(128)(4,1)}), s8[524288]{0:T(1024)(128)(4,1)S(1)}, s32[]{:S(2)}) async-start(s8[4718592]{0:T(1024)(128)(4,1)} %bitcast.147), calls=%async_computation.2 | async-start | bytes 1048576
  437.1 61.4 %slice-start.6 = ((s8[4718592]{0:T(1024)(128)(4,1)}), s8[4194304]{0:T(1024)(128)(4,1)S(1)}, s32[]{:S(2)}) async-start(s8[4718592]{0:T(1024)(128)(4,1)} %bitcast.151), calls=%async_computation.6 | async-start | bytes 8388608
  456.8 8.3 %collective-permute-start.1 = (bf16[1,64,1536]{2,1,0:T(8,128)(2,1)}, bf16[1,64,1536]{2,1,0:T(8,128)(2,1)S(1)}, u32[]{:S(2)}, u32[]{:S(2)}) collective-permute-start(bf16[1,64,1536]{2,1,0:T(8,128)(2,1)} %bitcast.132), channel_id=1, source_target_pairs={{0,16},{1,17},{2,18},{3,19},{4,20},{5,21},{6,22},{7,23},{8,24},{9,... | collective-permute-start | bytes 589832 | tf_op jit(solution)/shard_map/ppermute | solution.py:439
  483.3 12.8 %copy-start.5 = (bf16[256,1536]{1,0:T(8,128)(2,1)S(1)}, bf16[256,1536]{1,0:T(8,128)(2,1)}, u32[]{:S(2)}) copy-start(bf16[256,1536]{1,0:T(8,128)(2,1)} %shard_map.90) | copy-start | bytes 2359300
  483.4 12.8 %slice-start.3 = ((s8[4718592]{0:T(1024)(128)(4,1)}), s8[4194304]{0:T(1024)(128)(4,1)S(1)}, s32[]{:S(2)}) async-start(s8[4718592]{0:T(1024)(128)(4,1)} %bitcast.147), calls=%async_computation.3 | async-start | bytes 8388608
  483.4 15.2 %slice-start.7 = ((s8[4718592]{0:T(1024)(128)(4,1)}), s8[524288]{0:T(1024)(128)(4,1)S(1)}, s32[]{:S(2)}) async-start(s8[4718592]{0:T(1024)(128)(4,1)} %bitcast.151), calls=%async_computation.7 | async-start | bytes 1048576
  496.2 4.6 slice-start.12
  498.5 2.3 slice-start.13
  597.1 71.9 %slice-start.16 = ((s8[4718592]{0:T(1024)(128)(4,1)}), s8[524288]{0:T(1024)(128)(4,1)S(1)}, s32[]{:S(2)}) async-start(s8[4718592]{0:T(1024)(128)(4,1)} %bitcast.161), calls=%async_computation.16 | async-start | bytes 1048576
  658.9 10.1 %slice-start.17 = ((s8[4718592]{0:T(1024)(128)(4,1)}), s8[4194304]{0:T(1024)(128)(4,1)S(1)}, s32[]{:S(2)}) async-start(s8[4718592]{0:T(1024)(128)(4,1)} %bitcast.161), calls=%async_computation.17 | async-start | bytes 8388608
  658.9 10.1 %copy-start.8 = (bf16[256,1536]{1,0:T(8,128)(2,1)S(1)}, bf16[256,1536]{1,0:T(8,128)(2,1)}, u32[]{:S(2)}) copy-start(bf16[256,1536]{1,0:T(8,128)(2,1)} %get-tuple-element.15) | copy-start | bytes 2359300
  669.0 16.2 %copy-start.1 = (bf16[64,1536]{1,0:T(8,128)(2,1)S(1)}, bf16[64,1536]{1,0:T(8,128)(2,1)}, u32[]{:S(2)}) copy-start(bf16[64,1536]{1,0:T(8,128)(2,1)} %shard_map.85) | copy-start | bytes 589828
  669.0 16.2 %copy-start.2 = (bf16[64,1536]{1,0:T(8,128)(2,1)S(1)}, bf16[64,1536]{1,0:T(8,128)(2,1)}, u32[]{:S(2)}) copy-start(bf16[64,1536]{1,0:T(8,128)(2,1)} %shard_map.89) | copy-start | bytes 589828
where the time goes:
time: 694 us; the launch traced here: 687 us
  Pallas kernels  526 us (76%)
  matrix products  104 us (15%)
  other arithmetic  30.6 us (4%)
  waiting for transfers between devices  14.4 us (2%)
  local copies, waits for them, and re-layouts  8.38 us (1%)
    pallas_call x3, Pallas kernels, reduce_line(): pl.pallas_call(functools.partial(reduce_kernel, rows), out_shape=jax.Shap...  249 us
    pallas_call x3, Pallas kernels, spread_line(): pl.pallas_call(functools.partial(spread_kernel, rows), out_shape=[jax.Sha...  181 us
    dot_general x12, matrix products, line_layer(): jnp.dot(gathered, w, preferred_element_type=jnp.float32)  61.7 us
    pallas_call x3, Pallas kernels, norm_gather(): pl.pallas_call(functools.partial(norm_kernel, rows, cols), out_shape=jax....  53.6 us
    pallas_call x3, Pallas kernels, finish(): pl.pallas_call(functools.partial(finish_kernel, cols), out_shape=jax.Shap...  42.6 us
    dot_general x3, matrix products, line_layer(): jnp.dot(act_full, wdown, preferred_element_type=jnp.float32)  30 us
    convert_element_type x3, other arithmetic, line_layer(): act = jax.nn.gelu(pre, approximate=False).astype(jnp.bfloat16)  25.7 us
    ppermute x2, waiting for transfers between devices, passed_along(): lax.ppermute(value, axis, [(source, source + steps) for source in range(f...  14.4 us
  transfers between devices with their start and end apart: 2, of which 2 were waited for; matrix products, arithmetic and copies ran while one was open for 0% of the time, Pallas kernels for 0%

commit v1 on v0

v1 whole, which is shorter than its diff:
```python
import functools
from typing import NamedTuple

import jax
import jax.numpy as jnp
from jax import lax
from jax.experimental import pallas as pl
from jax.experimental.pallas import tpu as pltpu
from jax.sharding import PartitionSpec as P

D = 6144
HEADS = 48
HEAD = D // HEADS


EPS = 1e-06
MESH = pl.DeviceIdType.MESH
VMEM_BYTES = 60 * 1024 * 1024
LAG = 2
RUNG = 2
SLOTS = 3
PAIR_LAG = 2
CROSS_LAG = 5


class Plan(NamedTuple):
    owner: int
    last: bool
    rows: int
    cols: int
    images: int
    heads: tuple
    units: tuple

    def chunks(self, half):
        return 3 * self.heads[half] + self.units[half]


def plan_of(x, wq, wup, owner, last):
    heads = wq.shape[1] // HEAD // 2
    units = wup.shape[1] // HEAD // 2
    far_heads = heads // 2
    far_units = units * 5 // 12
    return Plan(
        owner,
        last,
        lax.axis_size("row"),
        lax.axis_size("col"),
        x.shape[0],
        (heads - far_heads, far_heads),
        (units - far_units, far_units),
    )


def greet_peers(axes):
    barrier = pltpu.get_barrier_semaphore()
    total = 0
    for axis, count in axes:
        me = lax.axis_index(axis)
        for step in range(1, count):
            pl.semaphore_signal(
                barrier, inc=1, device_id={axis: lax.rem(me + step, count)}, device_id_type=MESH
            )
            total += 1
    pl.semaphore_wait(barrier, total)


def both(first, *rest):
    for other in rest:
        first = jnp.logical_and(first, other)
    return first


def layer_kernel(
    plan,
    x_ref,
    gain_ref,
    wq_ref,
    wk_ref,
    wv_ref,
    wup_ref,
    wout_ref,
    wdown_ref,
    out_ref,
    stats,
    full,
    part,
    away,
    held,
    act,
    far,
    wbuf,
    dbuf,
    acc,
    own,
    pair_out,
    pair_in,
    cross_out,
    cross_in,
    stat_sem,
    gather_sem,
    wsem,
    dsem,
    reduce_sem,
    spread_sem,
    rung_sem,
    far_sem,
    pair_sem,
    cross_sem,
    pass_sem,
):
    rows, cols, images = plan.rows, plan.cols, plan.images
    last = rows - 1
    per_image = max(plan.chunks(0), plan.chunks(1))
    count = images * per_image
    row, col, section = lax.axis_index("row"), lax.axis_index("col"), lax.axis_index("section")
    is_owner = section == plan.owner
    is_far = jnp.logical_not(is_owner)
    chips = cols // 2
    chip, core = lax.div(col, 2), lax.rem(col, 2)
    partner = 2 * chip + (1 - core)
    patches, width = x_ref.shape[1], x_ref.shape[2]
    total_rows = patches * cols
    entry = jnp.where(is_owner, 0, RUNG)
    my_heads = jnp.where(is_owner, plan.heads[0], plan.heads[1])
    my_chunks = jnp.where(is_owner, plan.chunks(0), plan.chunks(1))
    depth = 2 * RUNG + 2 * LAG * last
    greet_peers((("row", rows), ("col", cols), ("section", 2)))

    def remote(src, dst, send, recv, **where):
        return pltpu.make_async_remote_copy(
            src_ref=src, dst_ref=dst, send_sem=send, recv_sem=recv, device_id=where, device_id_type=MESH
        )

    def chip_at(step):
        return lax.rem(chip + step, chips)

    def chip_behind(step):
        return lax.rem(chip + chips - step, chips)

    def gather_cross(image, step):
        place = full.at[image, col]
        return remote(
            place,
            place,
            gather_sem.at[0, 0, image, step],
            gather_sem.at[0, 1, image, step],
            col=2 * chip_at(step) + core,
        )

    def gather_pair(image, step):
        place = full.at[image, 2 * chip_behind(step) + core]
        return remote(
            place, place, gather_sem.at[1, 0, image, step], gather_sem.at[1, 1, image, step], col=partner
        )

    def relay(image):
        for step in range(1, chips):
            gather_cross(image, step).wait_recv()
            gather_pair(image, step).start()

    def gathered(image):
        for step in range(chips):
            gather_pair(image, step).wait_recv()

    def chunk_kind(half, j):
        heads = 3 * plan.heads[half]
        return j < heads, lax.rem(j, 3), lax.div(j, 3), j - heads

    def head_base(half, side):
        return side * plan.heads[0] if half == 0 else 2 * plan.heads[0] + side * plan.heads[1]

    def unit_base(half, side):
        return side * plan.units[0] if half == 0 else 2 * plan.units[0] + side * plan.units[1]

    def in_copy(ref, half, side, slot, block):
        start = pl.multiple_of(block * HEAD, HEAD)
        return pltpu.make_async_copy(
            ref.at[:, pl.ds(start, HEAD)],
            wbuf.at[slot, half, :, pl.ds(side * HEAD, HEAD)],
            wsem.at[slot, half, side],
        )

    def out_copy(ref, half, side, slot, block):
        start = pl.multiple_of(block * HEAD, HEAD)
        return pltpu.make_async_copy(
            ref.at[pl.ds(start, HEAD), :],
            dbuf.at[slot, half, pl.ds(side * HEAD, HEAD), :],
            dsem.at[slot, half, side],
        )

    def fetch_in(c):
        j, slot = lax.rem(c, per_image), lax.rem(c, SLOTS)
        for half in range(2):
            is_head, kind, head, unit = chunk_kind(half, j)
            for index, ref in enumerate((wq_ref, wk_ref, wv_ref)):

                @pl.when(both(is_head, kind == index))
                def _():
                    for side in range(2):
                        in_copy(ref, half, side, slot, head_base(half, side) + head).start()

            @pl.when(both(jnp.logical_not(is_head), j < plan.chunks(half)))
            def _():
                for side in range(2):
                    in_copy(wup_ref, half, side, slot, unit_base(half, side) + unit).start()

    def yields(half, j):
        is_head, kind, _, _ = chunk_kind(half, j)
        return jnp.logical_or(both(is_head, kind == 2), both(jnp.logical_not(is_head), j < plan.chunks(half)))

    def fetch_out(c):
        j, slot = lax.rem(c, per_image), lax.rem(c, SLOTS)
        for half in range(2):
            is_head, kind, head, unit = chunk_kind(half, j)

            @pl.when(both(is_head, kind == 2))
            def _():
                for side in range(2):
                    out_copy(wout_ref, half, side, slot, head_base(half, side) + head).start()

            @pl.when(both(jnp.logical_not(is_head), j < plan.chunks(half)))
            def _():
                for side in range(2):
                    out_copy(wdown_ref, half, side, slot, unit_base(half, side) + unit).start()

    def rung_copy(c):
        return remote(away.at[c], part.at[c], rung_sem.at[0, c], rung_sem.at[1, c], section=1 - section)

    def far_copy(side, c):
        return remote(
            act.at[side, c],
            far.at[side, c],
            far_sem.at[0, side, c],
            far_sem.at[1, side, c],
            section=1 - section,
        )

    def toward(side):
        return jnp.minimum(row + 1, last) if side == 1 else jnp.maximum(row - 1, 0)

    def hops_of(side):
        return row if side == 1 else last - row

    def reduce_copy(side, c, own_part):
        src = part.at[c, side] if own_part else held.at[side, c]
        return remote(
            src, held.at[side, c], reduce_sem.at[0, side, c], reduce_sem.at[1, side, c], row=toward(side)
        )

    def spread_copy(side, c):
        place = act.at[side, c]
        return remote(
            place, place, spread_sem.at[0, side, c], spread_sem.at[1, side, c], row=toward(1 - side)
        )

    def project(c):
        image, j, slot = lax.div(c, per_image), lax.rem(c, per_image), lax.rem(c, SLOTS)
        for half in range(2):

            @pl.when(j < plan.chunks(half))
            def _():
                for side in range(2):
                    in_copy(wup_ref, half, side, slot, 0).wait()
                value = jnp.dot(
                    full[image].reshape(total_rows, width),
                    wbuf[slot, half],
                    preferred_element_type=jnp.float32,
                ).astype(jnp.bfloat16)
                target = part if half == 0 else away
                target[c, 0] = value[:, :HEAD]
                target[c, 1] = value[:, HEAD:]

        @pl.when(j < plan.chunks(1))
        def _():
            rung_copy(c).start()

        @pl.when(c + SLOTS < count)
        def _():
            fetch_in(c + SLOTS)

    def attend(side, c, value):
        scores = lax.dot_general(
            held[side, c - 2], held[side, c - 1], (((1,), (1,)), ((), ())), preferred_element_type=jnp.float32
        ) / (float(HEAD) ** 0.5)
        expo = jnp.exp(scores - jnp.max(scores, axis=-1, keepdims=True))
        probs = (expo / jnp.sum(expo, axis=-1, keepdims=True)).astype(jnp.bfloat16)
        return jnp.dot(probs, value, preferred_element_type=jnp.float32).astype(jnp.bfloat16)

    def finish_sum(side, c, j):
        total = part[c, side].astype(jnp.float32) + held[side, c].astype(jnp.float32)
        is_head, kind = j < 3 * my_heads, lax.rem(j, 3)

        @pl.when(is_head)
        def _():
            held[side, c] = total.astype(jnp.bfloat16)

        @pl.when(both(is_head, kind == 2))
        def _():
            act[side, c] = attend(side, c, total.astype(jnp.bfloat16))

        @pl.when(jnp.logical_not(is_head))
        def _():
            act[side, c] = (0.5 * total * (1.0 + lax.erf(total * (0.5**0.5)))).astype(jnp.bfloat16)

    def my_yield(j):
        is_head, kind = j < 3 * my_heads, lax.rem(j, 3)
        return jnp.logical_or(both(is_head, kind == 2), both(jnp.logical_not(is_head), j < my_chunks))

    def in_range(c):
        return both(c >= 0, c < count)

    def spread_stage(s):
        for side in range(2):
            dist = hops_of(1 - side)
            c = s - entry - LAG * (last + dist)
            j = lax.rem(c, per_image)

            @pl.when(both(dist > 0, in_range(c), my_yield(j)))
            def _():
                spread_copy(side, c).wait_recv()

                @pl.when(dist < last)
                def _():
                    spread_copy(side, c).start()

                @pl.when(is_far)
                def _():
                    far_copy(side, c).start()

    def reduce_stage(s):
        c_rung = s - RUNG

        @pl.when(both(is_far, in_range(c_rung), lax.rem(c_rung, per_image) < plan.chunks(1)))
        def _():
            rung_copy(c_rung).wait_recv()

        for side in range(2):
            hops = hops_of(side)
            c = s - entry - LAG * hops
            live = both(in_range(c), lax.rem(c, per_image) < my_chunks)

            @pl.when(both(live, hops == 0))
            def _():
                reduce_copy(side, c, True).start()

            @pl.when(both(live, hops > 0, hops < last))
            def _():
                reduce_copy(side, c, False).wait_recv()
                held[side, c] = (
                    part[c, side].astype(jnp.float32) + held[side, c].astype(jnp.float32)
                ).astype(jnp.bfloat16)
                reduce_copy(side, c, False).start()

    def root_stage(s):
        side = jnp.where(row == 0, 0, 1)
        c = s - entry - LAG * last
        j = lax.rem(c, per_image)

        @pl.when(both(jnp.logical_or(row == 0, row == last), in_range(c), j < my_chunks))
        def _():
            for which in range(2):

                @pl.when(side == which)
                def _():
                    reduce_copy(which, c, False).wait_recv()

            finish_sum(side, c, j)

            @pl.when(my_yield(j))
            def _():
                for which in range(2):

                    @pl.when(side == which)
                    def _():
                        spread_copy(which, c).start()

                        @pl.when(is_far)
                        def _():
                            far_copy(which, c).start()

    def down_stage(s):
        c = s - depth

        @pl.when(in_range(c))
        def _():
            j, slot = lax.rem(c, per_image), lax.rem(c, SLOTS)

            @pl.when(j == 0)
            def _():
                acc[...] = jnp.zeros_like(acc)

            for half in range(2):

                @pl.when(yields(half, j))
                def _():
                    source = act if half == 0 else far
                    for side in range(2):
                        if half == 1:
                            far_copy(side, c).wait_recv()
                        out_copy(wdown_ref, half, side, slot, 0).wait()
                    lhs = jnp.concatenate([source[0, c], source[1, c]], axis=1)
                    acc[...] += jnp.dot(lhs, dbuf[slot, half], preferred_element_type=jnp.float32).reshape(
                        acc.shape
                    )

            @pl.when(c + SLOTS < count)
            def _():
                fetch_out(c + SLOTS)

    def pair_copy(image):
        return remote(
            pair_out.at[image], pair_in.at[image], pair_sem.at[0, image], pair_sem.at[1, image], col=partner
        )

    def cross_copy(image, step):
        return remote(
            cross_out.at[image, step],
            cross_in.at[image, step],
            cross_sem.at[0, image, step],
            cross_sem.at[1, image, step],
            col=2 * chip_at(step) + core,
        )

    def pass_copy(image):
        return remote(
            out_ref.at[image],
            out_ref.at[image],
            pass_sem.at[0, image],
            pass_sem.at[1, image],
            section=1 - section,
        )

    def ended(s, lag):
        done = s - depth - lag + 1
        return both(done > 0, done <= count, lax.rem(done, per_image) == 0), lax.div(done, per_image) - 1

    def close_stage(s):
        at_end, image = ended(s, 0)

        @pl.when(at_end)
        def _():
            for step in range(chips):
                theirs = 2 * chip_at(step)
                pair_out[image, step] = acc[theirs + (1 - core)].astype(jnp.bfloat16)
                own[step] = acc[theirs + core]
            pair_copy(image).start()

        at_pair, image_pair = ended(s, PAIR_LAG)

        @pl.when(at_pair)
        def _():
            pair_copy(image_pair).wait_recv()
            for step in range(1, chips):
                cross_out[image_pair, step] = (
                    own[step] + pair_in[image_pair, step].astype(jnp.float32)
                ).astype(jnp.bfloat16)
                cross_copy(image_pair, step).start()
            own[0] = own[0] + pair_in[image_pair, 0].astype(jnp.float32)

        at_cross, image_cross = ended(s, PAIR_LAG + CROSS_LAG)

        @pl.when(at_cross)
        def _():
            total = own[0]
            for step in range(1, chips):
                cross_copy(image_cross, step).wait_recv()
                total = total + cross_in[image_cross, step].astype(jnp.float32)
            out_ref[image_cross] = (x_ref[image_cross].astype(jnp.float32) + total).astype(jnp.bfloat16)
            if not plan.last:
                pass_copy(image_cross).start()

    @pl.when(is_owner)
    def _():
        for c in range(SLOTS):
            fetch_in(jnp.int32(c))
            fetch_out(jnp.int32(c))
        xf = x_ref[...].reshape(images * patches, width).astype(jnp.float32)
        total = jnp.sum(xf, axis=-1, keepdims=True)
        square = jnp.sum(xf * xf, axis=-1, keepdims=True)
        lane = lax.broadcasted_iota(jnp.int32, (images * patches, 128), 1)
        stats[0] = jnp.where(lane < 64, total, square)
        copies = []
        for step in range(1, rows):
            copy = remote(
                stats.at[0],
                stats.at[step],
                stat_sem.at[0, step],
                stat_sem.at[1, step],
                row=lax.rem(row + step, rows),
            )
            copy.start()
            copies.append(copy)
        for copy in copies:
            copy.wait()
        sums = stats[0]
        for step in range(1, rows):
            sums = sums + stats[step]
        mean = sums[:, 0:1] / D
        var = jnp.maximum(sums[:, 64:65] / D - mean * mean, 0.0)
        normed = ((xf - mean) * lax.rsqrt(var + EPS) * gain_ref[...]).astype(jnp.bfloat16)
        for image in range(images):
            full[image, col] = normed[image * patches : (image + 1) * patches]
            for step in range(1, chips):
                gather_cross(image, step).start()
            gather_pair(image, 0).start()
        relay(0)
        gathered(0)
        project(jnp.int32(0))

    def step(s, carry):
        spread_stage(s)
        reduce_stage(s)
        root_stage(s)

        @pl.when(is_owner)
        def _():
            for image in range(1, images):

                @pl.when(s == image * per_image - per_image // 2)
                def _():
                    relay(image)

                @pl.when(s == image * per_image - 1)
                def _():
                    gathered(image)

            @pl.when(s + 1 < count)
            def _():
                project(s + 1)

            down_stage(s)
            close_stage(s)

        return carry

    lax.fori_loop(0, count + depth + PAIR_LAG + CROSS_LAG, step, 0)

    def drain(c, carry):
        j = lax.rem(c, per_image)
        for side in range(2):
            hops = hops_of(side)

            @pl.when(both(j < my_chunks, hops < last))
            def _():
                reduce_copy(side, c, False).wait_send()

            @pl.when(my_yield(j))
            def _():
                @pl.when(hops_of(1 - side) < last)
                def _():
                    spread_copy(side, c).wait_send()

                @pl.when(is_far)
                def _():
                    far_copy(side, c).wait_send()

        @pl.when(both(is_owner, j < plan.chunks(1)))
        def _():
            rung_copy(c).wait_send()

        return carry

    lax.fori_loop(0, count, drain, 0)

    @pl.when(is_owner)
    def _():
        for image in range(images):
            for step in range(chips):
                gather_pair(image, step).wait_send()
                if step:
                    gather_cross(image, step).wait_send()
                    cross_copy(image, step).wait_send()
            pair_copy(image).wait_send()
            if not plan.last:
                pass_copy(image).wait_send()

    if not plan.last:

        @pl.when(is_far)
        def _():
            for image in range(images):
                pass_copy(image).wait_recv()


def fused_layer(x, weights, owner, last):
    gain, wq, wk, wv, wup, wout, wdown = weights
    plan = plan_of(x, wq, wup, owner, last)
    images, patches, width = x.shape
    rows, cols = plan.rows, plan.cols
    chips = cols // 2
    count = images * max(plan.chunks(0), plan.chunks(1))
    total_rows = patches * cols
    bf16, f32 = jnp.bfloat16, jnp.float32
    dma = pltpu.SemaphoreType.DMA
    vmem = pl.BlockSpec(memory_space=pltpu.VMEM)
    hbm = pl.BlockSpec(memory_space=pl.ANY)
    return pl.pallas_call(
        functools.partial(layer_kernel, plan),
        out_shape=jax.ShapeDtypeStruct(x.shape, bf16),
        in_specs=[vmem, vmem] + [hbm] * 6,
        out_specs=vmem,
        scratch_shapes=[
            pltpu.VMEM((rows, images * patches, 128), f32),
            pltpu.VMEM((images, cols, patches, width), bf16),
            pltpu.VMEM((count, 2, total_rows, HEAD), bf16),
            pltpu.VMEM((count, 2, total_rows, HEAD), bf16),
            pltpu.VMEM((2, count, total_rows, HEAD), bf16),
            pltpu.VMEM((2, count, total_rows, HEAD), bf16),
            pltpu.VMEM((2, count, total_rows, HEAD), bf16),
            pltpu.VMEM((SLOTS, 2, width, 2 * HEAD), bf16),
            pltpu.VMEM((SLOTS, 2, 2 * HEAD, width), bf16),
            pltpu.VMEM((cols, patches, width), f32),
            pltpu.VMEM((chips, patches, width), f32),
            pltpu.VMEM((images, chips, patches, width), bf16),
            pltpu.VMEM((images, chips, patches, width), bf16),
            pltpu.VMEM((images, chips, patches, width), bf16),
            pltpu.VMEM((images, chips, patches, width), bf16),
            dma((2, rows)),
            dma((2, 2, images, chips)),
            dma((SLOTS, 2, 2)),
            dma((SLOTS, 2, 2)),
            dma((2, 2, count)),
            dma((2, 2, count)),
            dma((2, count)),
            dma((2, 2, count)),
            dma((2, images)),
            dma((2, images, chips)),
            dma((2, images)),
        ],
        compiler_params=pltpu.CompilerParams(
            collective_id=owner, has_side_effects=True, vmem_limit_bytes=VMEM_BYTES
        ),
    )(x, gain[None], wq, wk, wv, wup, wout, wdown)


def fits(x, wq, wup):
    rows, cols = lax.axis_size("row"), lax.axis_size("col")
    heads, units = wq.shape[1] // HEAD, wup.shape[1] // HEAD
    return (
        lax.axis_size("section") == 2
        and rows > 1
        and cols % 2 == 0
        and x.shape[1] % 16 == 0
        and wq.shape[1] % (2 * HEAD) == 0
        and wup.shape[1] % (2 * HEAD) == 0
        and heads >= 4
        and units >= 6
    )


def passed_along(value, axis, steps):
    count = lax.axis_size(axis)
    first, last = (max(0, -steps), min(count, count - steps))
    return lax.ppermute(value, axis, [(source, source + steps) for source in range(first, last)])


def layer(x, weights):
    gain, wq, wk, wv, wup, wout, wdown = weights
    xf = x.astype(jnp.float32)
    sums, squares = lax.psum((jnp.sum(xf, axis=-1), jnp.sum(xf * xf, axis=-1)), "row")
    mean = (sums / D)[..., None]
    var = jnp.maximum((squares / D)[..., None] - mean * mean, 0.0)
    normed = ((xf - mean) * lax.rsqrt(var + EPS) * gain).astype(jnp.bfloat16)
    gathered = lax.all_gather(normed, "col", axis=1, tiled=True)
    part_q = jnp.dot(gathered, wq, preferred_element_type=jnp.float32)
    part_k = jnp.dot(gathered, wk, preferred_element_type=jnp.float32)
    part_v = jnp.dot(gathered, wv, preferred_element_type=jnp.float32)
    part_m = jnp.dot(gathered, wup, preferred_element_type=jnp.float32)
    query, keyed, valued, pre = (
        lax.psum_scatter(
            part_q.astype(jnp.bfloat16), "row", scatter_dimension=1, tiled=True
        ).astype(jnp.float32),
        lax.psum_scatter(
            part_k.astype(jnp.bfloat16), "row", scatter_dimension=1, tiled=True
        ).astype(jnp.float32),
        lax.psum_scatter(
            part_v.astype(jnp.bfloat16), "row", scatter_dimension=1, tiled=True
        ).astype(jnp.float32),
        lax.psum_scatter(
            part_m.astype(jnp.bfloat16), "row", scatter_dimension=1, tiled=True
        ).astype(jnp.float32),
    )
    act = jax.nn.gelu(pre, approximate=False).astype(jnp.bfloat16)
    query = query.astype(jnp.bfloat16)
    keyed = keyed.astype(jnp.bfloat16)
    valued = valued.astype(jnp.bfloat16)
    all_keys, all_values = (
        lax.all_gather(keyed, "row", axis=1, tiled=True),
        lax.all_gather(valued, "row", axis=1, tiled=True),
    )
    head_dim = D // HEADS
    local_heads = query.shape[2] // head_dim
    images = query.shape[0]
    qh = query.reshape(images, query.shape[1], local_heads, head_dim)
    kh = all_keys.reshape(images, all_keys.shape[1], local_heads, head_dim)
    vh = all_values.reshape(images, all_values.shape[1], local_heads, head_dim)
    scores = jnp.einsum("bqhd,bkhd->bhqk", qh, kh, preferred_element_type=jnp.float32) / jnp.sqrt(
        jnp.float32(head_dim)
    )
    scores = scores - jnp.max(scores, axis=-1, keepdims=True)
    expo = jnp.exp(scores)
    probs = (expo / jnp.sum(expo, axis=-1, keepdims=True)).astype(jnp.bfloat16)
    attn = jnp.einsum("bhqk,bkhd->bqhd", probs, vh, preferred_element_type=jnp.float32)
    attn = attn.reshape(query.shape).astype(jnp.bfloat16)
    attn_full, act_full = (
        lax.all_gather(attn, "row", axis=1, tiled=True),
        lax.all_gather(act, "row", axis=1, tiled=True),
    )
    mixed = jnp.dot(attn_full, wout, preferred_element_type=jnp.float32) + jnp.dot(
        act_full, wdown, preferred_element_type=jnp.float32
    )
    summed = lax.psum_scatter(
        mixed.astype(jnp.bfloat16), "col", scatter_dimension=1, tiled=True
    ).astype(jnp.float32)
    return (xf + summed).astype(jnp.bfloat16)


def pass_on(output):
    return passed_along(output, "section", 1)


def local(tokens, ln_gain, w_query, w_key, w_value, w_up, w_out, w_down):
    weights = (ln_gain[0], w_query[0], w_key[0], w_value[0], w_up[0], w_out[0], w_down[0])
    section = lax.axis_index("section")
    sections = lax.axis_size("section")
    if fits(tokens, w_query[0], w_up[0]):
        first = fused_layer(tokens, weights, 0, False)
        second = fused_layer(first, weights, 1, True)
        return jnp.where(section == 0, first, second)[None]
    result = jnp.zeros_like(tokens)
    images = tokens.shape[0]
    ticks = images + sections - 1
    inbox = jnp.zeros_like(tokens[:1])
    positions = jnp.arange(images, dtype=jnp.int32)
    for tick in range(ticks):
        fresh = tokens[min(tick, images - 1) : min(tick, images - 1) + 1]
        current = jnp.where(section == 0, fresh, inbox)
        output = layer(current, weights)
        slot = tick - section
        result = jnp.where((positions == slot)[:, None, None], output, result)
        if tick + 1 < ticks:
            inbox = pass_on(output)
    return result[None]


def solution(mesh):
    return jax.shard_map(
        local,
        mesh=mesh,
        in_specs=(
            P(None, "col", "row"),
            P("section", "row"),
            P("section", "row", "col"),
            P("section", "row", "col"),
            P("section", "row", "col"),
            P("section", "row", "col"),
            P("section", "col", "row"),
            P("section", "col", "row"),
        ),
        out_specs=P("section", None, "col", "row"),
        check_vma=False,
    )
```

time: 694 us -> 362 us (0.52); the launches traced: 687 us -> 362 us
  Pallas kernels: 526 us -> 361 us
  matrix products: 104 us -> 0 us
  other arithmetic: 30.6 us -> 1.8 us
  waiting for transfers between devices: 14.4 us -> 0 us
  local copies, waits for them, and re-layouts: 8.38 us -> 0.01 us
    pallas_call x12 -> x2, Pallas kernels: 526 us -> 361 us  [fused_layer(): pl.pallas_call(functools.partial(layer_kernel, plan), out_shape=jax.Shape...]
    dot_general x21 -> x0, matrix products: 102 us -> none  [the longest x12 61.7 us: line_layer(): jnp.dot(gathered, w, preferred_element_type=jnp.float32)]
    convert_element_type x3 -> x0, other arithmetic: 25.7 us -> none  [line_layer(): act = jax.nn.gelu(pre, approximate=False).astype(jnp.bfloat16)]
    ppermute x2 -> x0, waiting for transfers between devices: 14.4 us -> none  [passed_along(): lax.ppermute(value, axis, [(source, source + steps) for source in range(f...]
  transfers between devices with their start and end apart: 2 -> 0, of which waited for: 2 -> 0; matrix products, arithmetic and copies ran while one was open for 0% -> 0% of each run, Pallas kernels for 0% -> 0%
where the time goes in v1:
time: 362 us
  Pallas kernels  361 us (100%)
    pallas_call x2, Pallas kernels, fused_layer(): pl.pallas_call(functools.partial(layer_kernel, plan), out_shape=jax.Shape...  361 us

profile of v1, /device:TPU:5, one launch (start us, length us, event | category | flops | bytes accessed | tf_op | source)
XLA Modules:
  0.0 362.3 jit_solution(10975327928864244505)
XLA Ops:
  0.0 182.4 %shard_map.82.x_ref = bf16[2,64,1536]{2,1,0:T(8,128)(2,1)} custom-call(bf16[2,64,1536]{2,1,0:T(8,128)(2,1)} %x_ref.1, f32[1,1536]{1,0:T(1,128)} %gain_ref.3, bf16[1536,1536]{1,0:T(8,128)(2,1)} %bitcast.12, bf16[1536,1536]{1,0:T(8,128)(2,1)} %bitcast.14, bf16[1536,1536]{1,0:T(8,128)(2,1)} %bitcast.16, bf16[1536,6144]{1,0:T(8,128)(2,1)} %bitcast.8, ...), custom_call_target="tpu_custom_call" | custom-call | tf_op jit(solution)/shard_map/pallas_call | solution.py:598
  182.4 0.0 copy-start
  182.4 178.1 %shard_map.83 = bf16[2,64,1536]{2,1,0:T(8,128)(2,1)} custom-call(bf16[2,64,1536]{2,1,0:T(8,128)(2,1)} %shard_map.82.x_ref, f32[1,1536]{1,0:T(1,128)} %gain_ref.3, bf16[1536,1536]{1,0:T(8,128)(2,1)} %bitcast.13, bf16[1536,1536]{1,0:T(8,128)(2,1)} %bitcast.15, bf16[1536,1536]{1,0:T(8,128)(2,1)} %bitcast.17, bf16[1536,6144]{1,0:T(8,128)(2,1)} %bitcast.9, ...), custom_call_target="tpu_custom_call" | custom-call | tf_op jit(solution)/shard_map/pallas_call | solution.py:598
  360.5 0.0 copy-done
  360.6 1.8 select_bitcast_fusion
Async XLA Ops:
  182.4 178.1 %copy-start = (bf16[2,64,1536]{2,1,0:T(8,128)(2,1)S(1)}, bf16[2,64,1536]{2,1,0:T(8,128)(2,1)}, u32[]{:S(2)}) copy-start(bf16[2,64,1536]{2,1,0:T(8,128)(2,1)} %shard_map.82.x_ref) | copy-start | bytes 1179652

commit v2 on v1

v2 whole, which is shorter than its diff:
```python
import functools
from typing import NamedTuple

import jax
import jax.numpy as jnp
from jax import lax
from jax.experimental import pallas as pl
from jax.experimental.pallas import tpu as pltpu
from jax.sharding import PartitionSpec as P

D = 6144
HEADS = 48
HEAD = D // HEADS


EPS = 1e-06
MESH = pl.DeviceIdType.MESH
VMEM_BYTES = 67043328
LAG = 2
RUNG = 2
SLOTS = 3
PAIR_LAG = 2
CROSS_LAG = 3
PASS_LAG = 2
STAT_LAG = 2
RELAY_LAG = 2
GATHER_LAG = 1


class Plan(NamedTuple):
    rows: int
    cols: int
    images: int
    heads: tuple
    units: tuple

    def slots(self):
        return 3 * self.heads[0] + self.units[0]

    def group(self):
        return -(-self.slots() // self.heads[0])

    def quota(self, half):
        return -(-self.units[1] // self.heads[0]) if half else self.group() - 3

    def kind(self, half, j):
        group, pos = lax.div(j, self.group()), lax.rem(j, self.group())
        unit = group * self.quota(half) + pos - 3
        is_head = both(pos < 3, group < self.heads[half])
        is_unit = both(pos >= 3, pos < 3 + self.quota(half), unit < self.units[half])
        return is_head, is_unit, pos, group, unit, group * (3 + self.quota(half)) + pos

    def used(self):
        groups, quota = self.heads[0], self.quota(1)
        used = [(g, p) for g in range(self.heads[1]) for p in range(3)]
        used += [(u // quota, 3 + u % quota) for u in range(self.units[1])]
        return max(g * self.group() + p for g, p in used), max(g * (3 + quota) + p for g, p in used)


def plan_of(x, wq, wup):
    heads = wq.shape[1] // HEAD // 2
    units = wup.shape[1] // HEAD // 2
    far_heads = heads // 2
    far_units = units * 5 // 12
    return Plan(
        lax.axis_size("row"),
        lax.axis_size("col"),
        x.shape[0],
        (heads - far_heads, far_heads),
        (units - far_units, far_units),
    )


def greet_peers(axes):
    barrier = pltpu.get_barrier_semaphore()
    total = 0
    for axis, count in axes:
        me = lax.axis_index(axis)
        for step in range(1, count):
            pl.semaphore_signal(
                barrier, inc=1, device_id={axis: lax.rem(me + step, count)}, device_id_type=MESH
            )
            total += 1
    pl.semaphore_wait(barrier, total)


def both(first, *rest):
    for other in rest:
        first = jnp.logical_and(first, other)
    return first


def layers_kernel(
    plan,
    x_ref,
    gain_ref,
    wq_ref,
    wk_ref,
    wv_ref,
    wup_ref,
    wout_ref,
    wdown_ref,
    out_ref,
    inbox,
    stats,
    full,
    part_near,
    part_far,
    held_near,
    held_far,
    act_near,
    act_far,
    away,
    back,
    wbuf,
    dbuf,
    acc,
    pair_out,
    pair_in,
    cross_out,
    cross_in,
    stat_sem,
    gather_sem,
    wsem,
    dsem,
    reduce_near,
    reduce_far,
    spread_near,
    spread_far,
    rung_sem,
    back_sem,
    pair_sem,
    cross_sem,
    pass_sem,
):
    rows, cols, images = plan.rows, plan.cols, plan.images
    last = rows - 1
    per_image, per_far = plan.slots(), plan.used()[1] + 1
    count = images * per_image
    row, col, section = lax.axis_index("row"), lax.axis_index("col"), lax.axis_index("section")
    chips = cols // 2
    chip, core = lax.div(col, 2), lax.rem(col, 2)
    partner = 2 * chip + (1 - core)
    patches, width = x_ref.shape[1], x_ref.shape[2]
    total_rows = patches * cols
    line = 2 * LAG * last
    closing = max(per_image - 1, plan.used()[0] + 2 * RUNG) + line
    passed = closing + PAIR_LAG + CROSS_LAG
    arrive = passed + PASS_LAG
    second = arrive + STAT_LAG + RELAY_LAG + GATHER_LAG + 1
    base = (section * second, (1 - section) * second)
    entry = (0, RUNG)
    parts, helds, acts = (part_near, part_far), (held_near, held_far), (act_near, act_far)
    reduce_sems, spread_sems = (reduce_near, reduce_far), (spread_near, spread_far)
    greet_peers((("row", rows), ("col", cols), ("section", 2)))

    def remote(src, dst, send, recv, **where):
        return pltpu.make_async_remote_copy(
            src_ref=src, dst_ref=dst, send_sem=send, recv_sem=recv, device_id=where, device_id_type=MESH
        )

    def split(c):
        return lax.div(c, per_image), lax.rem(c, per_image)

    def far_place(c):
        image, j = split(c)
        return image * per_far + plan.kind(1, j)[5]

    def place_of(role, c):
        return c if role == 0 else far_place(c)

    def in_range(c):
        return both(c >= 0, c < count)

    def used(role, j):
        is_head, is_unit = plan.kind(role, j)[:2]
        return jnp.logical_or(is_head, is_unit)

    def yields(role, j):
        is_head, is_unit, pos = plan.kind(role, j)[:3]
        return jnp.logical_or(both(is_head, pos == 2), is_unit)

    def chip_at(step):
        return lax.rem(chip + step, chips)

    def chip_behind(step):
        return lax.rem(chip + chips - step, chips)

    def gather_cross(image, step):
        place = full.at[image, col]
        return remote(
            place,
            place,
            gather_sem.at[0, 0, image, step],
            gather_sem.at[0, 1, image, step],
            col=2 * chip_at(step) + core,
        )

    def gather_pair(image, step):
        place = full.at[image, 2 * chip_behind(step) + core]
        return remote(
            place, place, gather_sem.at[1, 0, image, step], gather_sem.at[1, 1, image, step], col=partner
        )

    def stat_copy(image, step):
        return remote(
            stats.at[image, 0],
            stats.at[image, step],
            stat_sem.at[0, image, step],
            stat_sem.at[1, image, step],
            row=lax.rem(row + step, rows),
        )

    def measure(image):
        xf = inbox[image].astype(jnp.float32)
        total = jnp.sum(xf, axis=-1, keepdims=True)
        square = jnp.sum(xf * xf, axis=-1, keepdims=True)
        lane = lax.broadcasted_iota(jnp.int32, (patches, 128), 1)
        stats[image, 0] = jnp.where(lane < 64, total, square)
        for step in range(1, rows):
            stat_copy(image, step).start()

    def normalize(image):
        sums = stats[image, 0]
        for step in range(1, rows):
            stat_copy(image, step).wait_recv()
            sums = sums + stats[image, step]
        mean = sums[:, 0:1] / D
        var = jnp.maximum(sums[:, 64:65] / D - mean * mean, 0.0)
        xf = inbox[image].astype(jnp.float32)
        full[image, col] = ((xf - mean) * lax.rsqrt(var + EPS) * gain_ref[...]).astype(jnp.bfloat16)
        for step in range(1, chips):
            gather_cross(image, step).start()
        gather_pair(image, 0).start()

    def relay(image):
        for step in range(1, chips):
            gather_cross(image, step).wait_recv()
            gather_pair(image, step).start()

    def gathered(image):
        for step in range(chips):
            gather_pair(image, step).wait_recv()

    def head_base(half, side):
        return side * plan.heads[0] if half == 0 else 2 * plan.heads[0] + side * plan.heads[1]

    def unit_base(half, side):
        return side * plan.units[0] if half == 0 else 2 * plan.units[0] + side * plan.units[1]

    def in_copy(ref, half, side, slot, block):
        start = pl.multiple_of(block * HEAD, HEAD)
        return pltpu.make_async_copy(
            ref.at[:, pl.ds(start, HEAD)],
            wbuf.at[slot, half, :, pl.ds(side * HEAD, HEAD)],
            wsem.at[slot, half, side],
        )

    def out_copy(ref, half, side, slot, block):
        start = pl.multiple_of(block * HEAD, HEAD)
        return pltpu.make_async_copy(
            ref.at[pl.ds(start, HEAD), :],
            dbuf.at[slot, half, pl.ds(side * HEAD, HEAD), :],
            dsem.at[slot, half, side],
        )

    def fetch_in(c):
        _, j = split(c)
        slot = lax.rem(c, SLOTS)
        for half in range(2):
            is_head, is_unit, kind, head, unit, _ = plan.kind(half, j)
            for index, ref in enumerate((wq_ref, wk_ref, wv_ref)):

                @pl.when(both(is_head, kind == index))
                def _():
                    for side in range(2):
                        in_copy(ref, half, side, slot, head_base(half, side) + head).start()

            @pl.when(is_unit)
            def _():
                for side in range(2):
                    in_copy(wup_ref, half, side, slot, unit_base(half, side) + unit).start()

    def fetch_out(half, c):
        _, j = split(c)
        slot = lax.rem(c, SLOTS)
        is_head, is_unit, kind, head, unit, _ = plan.kind(half, j)

        @pl.when(both(is_head, kind == 2))
        def _():
            for side in range(2):
                out_copy(wout_ref, half, side, slot, head_base(half, side) + head).start()

        @pl.when(is_unit)
        def _():
            for side in range(2):
                out_copy(wdown_ref, half, side, slot, unit_base(half, side) + unit).start()

    def rung_copy(place):
        return remote(
            away.at[place], part_far.at[place], rung_sem.at[0, place], rung_sem.at[1, place], section=1 - section
        )

    def back_copy(side, place):
        return remote(
            act_far.at[side, place],
            back.at[side, place],
            back_sem.at[0, side, place],
            back_sem.at[1, side, place],
            section=1 - section,
        )

    def toward(side):
        return jnp.minimum(row + 1, last) if side == 1 else jnp.maximum(row - 1, 0)

    def hops_of(side):
        return row if side == 1 else last - row

    def reduce_copy(role, side, place, own_part):
        held, sem = helds[role], reduce_sems[role]
        src = parts[role].at[place, side] if own_part else held.at[side, place]
        return remote(
            src, held.at[side, place], sem.at[0, side, place], sem.at[1, side, place], row=toward(side)
        )

    def spread_copy(role, side, place):
        here, sem = acts[role].at[side, place], spread_sems[role]
        return remote(here, here, sem.at[0, side, place], sem.at[1, side, place], row=toward(1 - side))

    def project(c):
        image, j = split(c)
        slot = lax.rem(c, SLOTS)
        for half in range(2):

            @pl.when(used(half, j))
            def _():
                for side in range(2):
                    in_copy(wup_ref, half, side, slot, 0).wait()
                value = jnp.dot(
                    full[image].reshape(total_rows, width),
                    wbuf[slot, half],
                    preferred_element_type=jnp.float32,
                ).astype(jnp.bfloat16)
                target, place = (part_near, c) if half == 0 else (away, far_place(c))
                target[place, 0] = value[:, :HEAD]
                target[place, 1] = value[:, HEAD:]
                if half == 1:
                    rung_copy(place).start()

        @pl.when(c + SLOTS < count)
        def _():
            fetch_in(c + SLOTS)

    def finish_sum(role, side, place, j):
        held, act = helds[role], acts[role]
        total = parts[role][place, side].astype(jnp.float32) + held[side, place].astype(jnp.float32)
        is_head, is_unit, kind = plan.kind(role, j)[:3]

        @pl.when(is_head)
        def _():
            held[side, place] = total.astype(jnp.bfloat16)

        @pl.when(both(is_head, kind == 2))
        def _():
            scores = lax.dot_general(
                held[side, place - 2],
                held[side, place - 1],
                (((1,), (1,)), ((), ())),
                preferred_element_type=jnp.float32,
            ) / (float(HEAD) ** 0.5)
            expo = jnp.exp(scores - jnp.max(scores, axis=-1, keepdims=True))
            probs = (expo / jnp.sum(expo, axis=-1, keepdims=True)).astype(jnp.bfloat16)
            mixed = jnp.dot(probs, total.astype(jnp.bfloat16), preferred_element_type=jnp.float32)
            act[side, place] = mixed.astype(jnp.bfloat16)

        @pl.when(is_unit)
        def _():
            act[side, place] = (0.5 * total * (1.0 + lax.erf(total * (0.5**0.5)))).astype(jnp.bfloat16)

    def spread_stage(role, s):
        for side in range(2):
            dist = hops_of(1 - side)
            c = s - base[role] - entry[role] - LAG * (last + dist)
            _, j = split(c)

            @pl.when(both(dist > 0, in_range(c), yields(role, j)))
            def _():
                place = place_of(role, c)
                spread_copy(role, side, place).wait_recv()

                @pl.when(dist < last)
                def _():
                    spread_copy(role, side, place).start()

                if role == 1:
                    back_copy(side, place).start()

    def reduce_stage(role, s):
        if role == 1:
            c_rung = s - base[role] - RUNG

            @pl.when(both(in_range(c_rung), used(1, split(c_rung)[1])))
            def _():
                rung_copy(far_place(c_rung)).wait_recv()

        for side in range(2):
            hops = hops_of(side)
            c = s - base[role] - entry[role] - LAG * hops
            live = both(in_range(c), used(role, split(c)[1]))

            @pl.when(both(live, hops == 0))
            def _():
                reduce_copy(role, side, place_of(role, c), True).start()

            @pl.when(both(live, hops > 0, hops < last))
            def _():
                place, held = place_of(role, c), helds[role]
                reduce_copy(role, side, place, False).wait_recv()
                held[side, place] = (
                    parts[role][place, side].astype(jnp.float32) + held[side, place].astype(jnp.float32)
                ).astype(jnp.bfloat16)
                reduce_copy(role, side, place, False).start()

    def root_stage(role, s):
        side = jnp.where(row == 0, 0, 1)
        c = s - base[role] - entry[role] - LAG * last
        _, j = split(c)

        @pl.when(both(jnp.logical_or(row == 0, row == last), in_range(c), used(role, j)))
        def _():
            place = place_of(role, c)
            for which in range(2):

                @pl.when(side == which)
                def _():
                    reduce_copy(role, which, place, False).wait_recv()

            finish_sum(role, side, place, j)

            @pl.when(yields(role, j))
            def _():
                for which in range(2):

                    @pl.when(side == which)
                    def _():
                        spread_copy(role, which, place).start()
                        if role == 1:
                            back_copy(which, place).start()

    def down_stage(half, s):
        c = s - base[0] - line - 2 * RUNG * half

        @pl.when(in_range(c))
        def _():
            image, j = split(c)
            slot = lax.rem(c, SLOTS)
            if half == 0:

                @pl.when(j == 0)
                def _():
                    acc[image] = jnp.zeros((cols, patches, width), jnp.float32)

            @pl.when(yields(half, j))
            def _():
                place, source = place_of(half, c), (act_near, back)[half]
                for side in range(2):
                    if half == 1:
                        back_copy(side, place).wait_recv()
                    out_copy(wdown_ref, half, side, slot, 0).wait()
                lhs = jnp.concatenate([source[0, place], source[1, place]], axis=1)
                acc[image] += jnp.dot(lhs, dbuf[slot, half], preferred_element_type=jnp.float32).reshape(
                    cols, patches, width
                )

            @pl.when(c + SLOTS < count)
            def _():
                fetch_out(half, c + SLOTS)

    def pair_copy(image):
        return remote(
            pair_out.at[image], pair_in.at[image], pair_sem.at[0, image], pair_sem.at[1, image], col=partner
        )

    def cross_copy(image, step):
        return remote(
            cross_out.at[image, step],
            cross_in.at[image, step],
            cross_sem.at[0, image, step],
            cross_sem.at[1, image, step],
            col=2 * chip_at(step) + core,
        )

    def pass_copy(image):
        return remote(
            out_ref.at[image], inbox.at[image], pass_sem.at[0, image], pass_sem.at[1, image], section=1 - section
        )

    def event(s, first):
        since = s - first
        return both(in_range(since), lax.rem(since, per_image) == 0), lax.div(since, per_image)

    def close_stage(s):
        ending = base[0] + closing
        at_end, image_end = event(s, ending)

        @pl.when(at_end)
        def _():
            for step in range(chips):
                theirs = 2 * chip_at(step) + (1 - core)
                pair_out[image_end, step] = acc[image_end, theirs].astype(jnp.bfloat16)
            pair_copy(image_end).start()

        at_pair, image_pair = event(s, ending + PAIR_LAG)

        @pl.when(at_pair)
        def _():
            pair_copy(image_pair).wait_recv()
            for step in range(1, chips):
                cross_out[image_pair, step] = (
                    acc[image_pair, 2 * chip_at(step) + core] + pair_in[image_pair, step].astype(jnp.float32)
                ).astype(jnp.bfloat16)
                cross_copy(image_pair, step).start()

        at_cross, image_cross = event(s, ending + PAIR_LAG + CROSS_LAG)

        @pl.when(at_cross)
        def _():
            total = acc[image_cross, col] + pair_in[image_cross, 0].astype(jnp.float32)
            for step in range(1, chips):
                cross_copy(image_cross, step).wait_recv()
                total = total + cross_in[image_cross, step].astype(jnp.float32)
            out_ref[image_cross] = (inbox[image_cross].astype(jnp.float32) + total).astype(jnp.bfloat16)

            @pl.when(section == 0)
            def _():
                pass_copy(image_cross).start()

    def open_stage(s):
        at_pass, image_pass = event(s, arrive)

        @pl.when(at_pass)
        def _():
            pass_copy(image_pass).wait_recv()
            measure(image_pass)

        at_stat, image_stat = event(s, arrive + STAT_LAG)

        @pl.when(at_stat)
        def _():
            normalize(image_stat)

        at_relay, image_relay = event(s, arrive + STAT_LAG + RELAY_LAG)

        @pl.when(at_relay)
        def _():
            relay(image_relay)

        at_full, image_full = event(s, second - 1)

        @pl.when(at_full)
        def _():
            gathered(image_full)

    for c in range(SLOTS):
        fetch_in(jnp.int32(c))
        for half in range(2):
            fetch_out(half, jnp.int32(c))

    @pl.when(section == 0)
    def _():
        inbox[...] = x_ref[...]
        for image in range(images):
            measure(image)
        for image in range(images):
            normalize(image)
        relay(0)
        gathered(0)

    def step(at, carry):
        s = at - 1
        for role in range(2):
            spread_stage(role, s)
        for role in range(2):
            reduce_stage(role, s)
        for role in range(2):
            root_stage(role, s)

        @pl.when(section == 0)
        def _():
            for image in range(1, images):

                @pl.when(s == image * per_image - per_image // 2)
                def _():
                    relay(image)

                @pl.when(s == image * per_image - 1)
                def _():
                    gathered(image)

        @pl.when(section == 1)
        def _():
            open_stage(s)

        c_next = s - base[0] + 1

        @pl.when(in_range(c_next))
        def _():
            project(c_next)

        for half in range(2):
            down_stage(half, s)
        close_stage(s)
        return carry

    steps = second + count - per_image + closing + PAIR_LAG + CROSS_LAG + 2
    lax.fori_loop(0, steps, step, 0)

    def drain(c, carry):
        _, j = split(c)
        for role in range(2):
            for side in range(2):

                @pl.when(both(used(role, j), hops_of(side) < last))
                def _():
                    reduce_copy(role, side, place_of(role, c), False).wait_send()

                @pl.when(both(yields(role, j), hops_of(1 - side) < last))
                def _():
                    spread_copy(role, side, place_of(role, c)).wait_send()

                if role == 1:

                    @pl.when(yields(role, j))
                    def _():
                        back_copy(side, far_place(c)).wait_send()

        @pl.when(used(1, j))
        def _():
            rung_copy(far_place(c)).wait_send()

        return carry

    lax.fori_loop(0, count, drain, 0)

    for image in range(images):
        for step in range(1, rows):
            stat_copy(image, step).wait_send()
        for step in range(chips):
            gather_pair(image, step).wait_send()
            if step:
                gather_cross(image, step).wait_send()
                cross_copy(image, step).wait_send()
        pair_copy(image).wait_send()

        @pl.when(section == 0)
        def _():
            pass_copy(image).wait_send()


def fused_layers(x, weights):
    gain, wq, wk, wv, wup, wout, wdown = weights
    plan = plan_of(x, wq, wup)
    images, patches, width = x.shape
    rows, cols = plan.rows, plan.cols
    chips = cols // 2
    near, far = images * plan.slots(), images * (plan.used()[1] + 1)
    total_rows = patches * cols
    bf16, f32 = jnp.bfloat16, jnp.float32
    dma = pltpu.SemaphoreType.DMA
    vmem = pl.BlockSpec(memory_space=pltpu.VMEM)
    hbm = pl.BlockSpec(memory_space=pl.ANY)
    return pl.pallas_call(
        functools.partial(layers_kernel, plan),
        out_shape=jax.ShapeDtypeStruct(x.shape, bf16),
        in_specs=[vmem, vmem] + [hbm] * 6,
        out_specs=vmem,
        scratch_shapes=[
            pltpu.VMEM(x.shape, bf16),
            pltpu.VMEM((images, rows, patches, 128), f32),
            pltpu.VMEM((images, cols, patches, width), bf16),
            pltpu.VMEM((near, 2, total_rows, HEAD), bf16),
            pltpu.VMEM((far, 2, total_rows, HEAD), bf16),
            pltpu.VMEM((2, near, total_rows, HEAD), bf16),
            pltpu.VMEM((2, far, total_rows, HEAD), bf16),
            pltpu.VMEM((2, near, total_rows, HEAD), bf16),
            pltpu.VMEM((2, far, total_rows, HEAD), bf16),
            pltpu.VMEM((far, 2, total_rows, HEAD), bf16),
            pltpu.VMEM((2, far, total_rows, HEAD), bf16),
            pltpu.VMEM((SLOTS, 2, width, 2 * HEAD), bf16),
            pltpu.VMEM((SLOTS, 2, 2 * HEAD, width), bf16),
            pltpu.VMEM((images, cols, patches, width), f32),
            pltpu.VMEM((images, chips, patches, width), bf16),
            pltpu.VMEM((images, chips, patches, width), bf16),
            pltpu.VMEM((images, chips, patches, width), bf16),
            pltpu.VMEM((images, chips, patches, width), bf16),
            dma((2, images, rows)),
            dma((2, 2, images, chips)),
            dma((SLOTS, 2, 2)),
            dma((SLOTS, 2, 2)),
            dma((2, 2, near)),
            dma((2, 2, far)),
            dma((2, 2, near)),
            dma((2, 2, far)),
            dma((2, far)),
            dma((2, 2, far)),
            dma((2, images)),
            dma((2, images, chips)),
            dma((2, images)),
        ],
        compiler_params=pltpu.CompilerParams(
            collective_id=0, has_side_effects=True, vmem_limit_bytes=VMEM_BYTES
        ),
    )(x, gain[None], wq, wk, wv, wup, wout, wdown)


def fits(x, wq, wup):
    rows, cols = lax.axis_size("row"), lax.axis_size("col")
    if lax.axis_size("section") != 2 or rows < 2 or cols % 2 or x.shape[1] % 16:
        return False
    if wq.shape[1] % (2 * HEAD) or wup.shape[1] % (2 * HEAD):
        return False
    plan = plan_of(x, wq, wup)
    if not plan.heads[1] or not plan.units[1] or plan.slots() < 12 or plan.quota(0) < 1:
        return False
    dealt = plan.quota(1) <= plan.quota(0) and plan.heads[0] * plan.quota(0) >= plan.units[0]
    return dealt and plan.used()[0] < plan.slots()


def passed_along(value, axis, steps):
    count = lax.axis_size(axis)
    first, last = (max(0, -steps), min(count, count - steps))
    return lax.ppermute(value, axis, [(source, source + steps) for source in range(first, last)])


def layer(x, weights):
    gain, wq, wk, wv, wup, wout, wdown = weights
    xf = x.astype(jnp.float32)
    sums, squares = lax.psum((jnp.sum(xf, axis=-1), jnp.sum(xf * xf, axis=-1)), "row")
    mean = (sums / D)[..., None]
    var = jnp.maximum((squares / D)[..., None] - mean * mean, 0.0)
    normed = ((xf - mean) * lax.rsqrt(var + EPS) * gain).astype(jnp.bfloat16)
    gathered = lax.all_gather(normed, "col", axis=1, tiled=True)
    part_q = jnp.dot(gathered, wq, preferred_element_type=jnp.float32)
    part_k = jnp.dot(gathered, wk, preferred_element_type=jnp.float32)
    part_v = jnp.dot(gathered, wv, preferred_element_type=jnp.float32)
    part_m = jnp.dot(gathered, wup, preferred_element_type=jnp.float32)
    query, keyed, valued, pre = (
        lax.psum_scatter(
            part_q.astype(jnp.bfloat16), "row", scatter_dimension=1, tiled=True
        ).astype(jnp.float32),
        lax.psum_scatter(
            part_k.astype(jnp.bfloat16), "row", scatter_dimension=1, tiled=True
        ).astype(jnp.float32),
        lax.psum_scatter(
            part_v.astype(jnp.bfloat16), "row", scatter_dimension=1, tiled=True
        ).astype(jnp.float32),
        lax.psum_scatter(
            part_m.astype(jnp.bfloat16), "row", scatter_dimension=1, tiled=True
        ).astype(jnp.float32),
    )
    act = jax.nn.gelu(pre, approximate=False).astype(jnp.bfloat16)
    query = query.astype(jnp.bfloat16)
    keyed = keyed.astype(jnp.bfloat16)
    valued = valued.astype(jnp.bfloat16)
    all_keys, all_values = (
        lax.all_gather(keyed, "row", axis=1, tiled=True),
        lax.all_gather(valued, "row", axis=1, tiled=True),
    )
    head_dim = D // HEADS
    local_heads = query.shape[2] // head_dim
    images = query.shape[0]
    qh = query.reshape(images, query.shape[1], local_heads, head_dim)
    kh = all_keys.reshape(images, all_keys.shape[1], local_heads, head_dim)
    vh = all_values.reshape(images, all_values.shape[1], local_heads, head_dim)
    scores = jnp.einsum("bqhd,bkhd->bhqk", qh, kh, preferred_element_type=jnp.float32) / jnp.sqrt(
        jnp.float32(head_dim)
    )
    scores = scores - jnp.max(scores, axis=-1, keepdims=True)
    expo = jnp.exp(scores)
    probs = (expo / jnp.sum(expo, axis=-1, keepdims=True)).astype(jnp.bfloat16)
    attn = jnp.einsum("bhqk,bkhd->bqhd", probs, vh, preferred_element_type=jnp.float32)
    attn = attn.reshape(query.shape).astype(jnp.bfloat16)
    attn_full, act_full = (
        lax.all_gather(attn, "row", axis=1, tiled=True),
        lax.all_gather(act, "row", axis=1, tiled=True),
    )
    mixed = jnp.dot(attn_full, wout, preferred_element_type=jnp.float32) + jnp.dot(
        act_full, wdown, preferred_element_type=jnp.float32
    )
    summed = lax.psum_scatter(
        mixed.astype(jnp.bfloat16), "col", scatter_dimension=1, tiled=True
    ).astype(jnp.float32)
    return (xf + summed).astype(jnp.bfloat16)


def pass_on(output):
    return passed_along(output, "section", 1)


def local(tokens, ln_gain, w_query, w_key, w_value, w_up, w_out, w_down):
    weights = (ln_gain[0], w_query[0], w_key[0], w_value[0], w_up[0], w_out[0], w_down[0])
    section = lax.axis_index("section")
    sections = lax.axis_size("section")
    if fits(tokens, w_query[0], w_up[0]):
        return fused_layers(tokens, weights)[None]
    result = jnp.zeros_like(tokens)
    images = tokens.shape[0]
    ticks = images + sections - 1
    inbox = jnp.zeros_like(tokens[:1])
    positions = jnp.arange(images, dtype=jnp.int32)
    for tick in range(ticks):
        fresh = tokens[min(tick, images - 1) : min(tick, images - 1) + 1]
        current = jnp.where(section == 0, fresh, inbox)
        output = layer(current, weights)
        slot = tick - section
        result = jnp.where((positions == slot)[:, None, None], output, result)
        if tick + 1 < ticks:
            inbox = pass_on(output)
    return result[None]


def solution(mesh):
    return jax.shard_map(
        local,
        mesh=mesh,
        in_specs=(
            P(None, "col", "row"),
            P("section", "row"),
            P("section", "row", "col"),
            P("section", "row", "col"),
            P("section", "row", "col"),
            P("section", "row", "col"),
            P("section", "col", "row"),
            P("section", "col", "row"),
        ),
        out_specs=P("section", None, "col", "row"),
        check_vma=False,
    )
```

time: 362 us -> 320 us (0.88)
  Pallas kernels: 361 us -> 318 us
    pallas_call x2 -> x1, Pallas kernels: 361 us -> 318 us  [fused_layers(): pl.pallas_call(functools.partial(layers_kernel, plan), out_shape=jax.Shap...]
where the time goes in v2:
time: 320 us
  Pallas kernels  318 us (99%)
    pallas_call x1, Pallas kernels, fused_layers(): pl.pallas_call(functools.partial(layers_kernel, plan), out_shape=jax.Shap...  318 us

profile of v2, /device:TPU:5, one launch (start us, length us, event | category | flops | bytes accessed | tf_op | source)
XLA Modules:
  0.0 319.7 jit_solution(4037103259500374712)
XLA Ops:
  0.0 317.9 %shard_map.82 = bf16[2,64,1536]{2,1,0:T(8,128)(2,1)} custom-call(bf16[2,64,1536]{2,1,0:T(8,128)(2,1)} %x_ref.1, f32[1,1536]{1,0:T(1,128)} %gain_ref.1, bf16[1536,1536]{1,0:T(8,128)(2,1)} %bitcast.9, bf16[1536,1536]{1,0:T(8,128)(2,1)} %bitcast.10, bf16[1536,1536]{1,0:T(8,128)(2,1)} %bitcast.11, bf16[1536,6144]{1,0:T(8,128)(2,1)} %bitcast.7, ...), custom_call_target="tpu_custom_call" | custom-call | tf_op jit(solution)/shard_map/pallas_call | solution.py:672
  317.9 1.8 copy.10

commit v3 on v2

--- a/solution.py
+++ b/solution.py
@@ -61,7 +61,7 @@
     heads = wq.shape[1] // HEAD // 2
     units = wup.shape[1] // HEAD // 2
     far_heads = heads // 2
-    far_units = units * 5 // 12
+    far_units = units // 2
     return Plan(
         lax.axis_size("row"),
         lax.axis_size("col"),

time: 320 us -> 334 us (1.044)
  Pallas kernels: 318 us -> 332 us
    pallas_call x1, Pallas kernels: 318 us -> 332 us  [fused_layers(): pl.pallas_call(functools.partial(layers_kernel, plan), out_shape=jax.Shap...]
where the time goes in v3:
time: 334 us
  Pallas kernels  332 us (99%)
    pallas_call x1, Pallas kernels, fused_layers(): pl.pallas_call(functools.partial(layers_kernel, plan), out_shape=jax.Shap...  332 us

profile of v3, /device:TPU:5, one launch (start us, length us, event | category | flops | bytes accessed | tf_op | source)
XLA Modules:
  0.0 334.2 jit_solution(13873387329296132586)
XLA Ops:
  0.0 332.4 %shard_map.82 = bf16[2,64,1536]{2,1,0:T(8,128)(2,1)} custom-call(bf16[2,64,1536]{2,1,0:T(8,128)(2,1)} %x_ref.1, f32[1,1536]{1,0:T(1,128)} %gain_ref.1, bf16[1536,1536]{1,0:T(8,128)(2,1)} %bitcast.9, bf16[1536,1536]{1,0:T(8,128)(2,1)} %bitcast.10, bf16[1536,1536]{1,0:T(8,128)(2,1)} %bitcast.11, bf16[1536,6144]{1,0:T(8,128)(2,1)} %bitcast.7, ...), custom_call_target="tpu_custom_call" | custom-call | tf_op jit(solution)/shard_map/pallas_call | solution.py:672
  332.4 1.8 copy.10
